TPU v7x, 32 devices: a whole 2x2x4 slice. The times are simulated.
32 devices in a mesh: rep: 4 (over x, y), dp: 8 (over z, core).
Axes of the slice: x: 2, y: 2, z: 4, core: 2. Of those that a mesh axis runs over, the one named last changes fastest.
Arguments:
- x: bfloat16 [32, 2048, 1024], P(('rep', 'dp')), parts along dimension 0
- dy: bfloat16 [32, 2048, 1024], P(('rep', 'dp')), parts along dimension 0
- w_gate: bfloat16 [2, 1024, 2816], replicated
- w_up: bfloat16 [2, 1024, 2816], replicated
- w_down: bfloat16 [2, 2816, 1024], replicated
- m_w_gate: float32 [2, 1024, 2816], P(None, 'dp')
- m_w_up: float32 [2, 1024, 2816], P(None, 'dp')
- m_w_down: float32 [2, 2816, 1024], P(None, 'dp')
- v_w_gate: float32 [2, 1024, 2816], P(None, 'dp')
- v_w_up: float32 [2, 1024, 2816], P(None, 'dp')
- v_w_down: float32 [2, 2816, 1024], P(None, 'dp')
Outputs:
- output 1: bfloat16 [8, 1024, 2816], P('rep'), parts along dimension 0
- output 2: bfloat16 [8, 1024, 2816], P('rep'), parts along dimension 0
- output 3: bfloat16 [8, 2816, 1024], P('rep'), parts along dimension 0
- output 4: float32 [8, 1024, 2816], P('rep', 'dp'), parts along dimension 0
- output 5: float32 [8, 1024, 2816], P('rep', 'dp'), parts along dimension 0
- output 6: float32 [8, 2816, 1024], P('rep', 'dp'), parts along dimension 0
- output 7: float32 [8, 1024, 2816], P('rep', 'dp'), parts along dimension 0
- output 8: float32 [8, 1024, 2816], P('rep', 'dp'), parts along dimension 0
- output 9: float32 [8, 2816, 1024], P('rep', 'dp'), parts along dimension 0
There are 4 independent parts. A program takes and returns all parts, laid end to end along the dimension named above; an argument that names none is the same for every part.
All inputs are finite; a program needn't handle non-finite values.
Results may differ from a plain program's by a relative error of at most 0.02.
Values are sent between devices in bfloat16 or wider.
A program may use at most 2 GiB of HBM per device.

v0:
```python
import jax
import jax.numpy as jnp
from jax import lax

NAMES = ("w_gate", "w_up", "w_down")


def matmul(a, w):
    return jnp.dot(a, w, preferred_element_type=jnp.float32).astype(jnp.bfloat16)


def normed(h):
    wide = h.astype(jnp.float32)
    scale = lax.rsqrt(jnp.mean(wide**2, -1, keepdims=True) + 1e-6)
    return (wide * scale).astype(jnp.bfloat16)


def layer(h, w):
    a = normed(h)
    gate = jnp.dot(a, w["w_gate"], preferred_element_type=jnp.float32)
    up = jnp.dot(a, w["w_up"], preferred_element_type=jnp.float32)
    return h + matmul((jax.nn.silu(gate) * up).astype(jnp.bfloat16), w["w_down"])


def adamw(w, m, v, g):
    m = 0.9 * m + 0.1 * g
    v = 0.95 * v + 0.05 * g * g
    step = m * lax.rsqrt(v + 1e-8) + 0.1 * w
    return (w - 0.02 * step).astype(jnp.bfloat16), m, v


def stack(weights, h):
    for number in range(weights["w_gate"].shape[0]):
        h = layer(h, {name: w[number] for name, w in weights.items()})
    return h


def solution(mesh):
    groups = mesh.shape["rep"]

    def step(x, dy, *arrays):
        weights, m, v = (arrays[i : i + 3] for i in (0, 3, 6))
        x, dy = (t.reshape(groups, -1, *t.shape[1:]) for t in (x, dy))

        def of_a_group(x, dy):
            _, back = jax.vjp(lambda w: stack(w, x), dict(zip(NAMES, weights, strict=True)))
            by_weights = back(dy)[0]
            gradients = [by_weights[name].astype(jnp.float32) for name in NAMES]
            new = [adamw(w.astype(jnp.float32), m, v, g) for w, m, v, g in zip(weights, m, v, gradients, strict=True)]
            return tuple(one[which] for which in range(3) for one in new)

        return tuple(t.reshape(-1, *t.shape[2:]) for t in jax.vmap(of_a_group)(x, dy))

    return step
```

profile of v0, /device:TPU:0, one launch (start us, length us, event | category | flops | bytes accessed | tf_op | source)
XLA Modules:
  0.0 1237.3 jit_solution(15001921468101397216)
XLA Ops:
  7.2 0.0 reduce-scatter.27.cloned.1.call-start
  7.2 3.1 fusion.35
  10.3 6.5 copy
  16.8 20.0 %fusion.67 = f32[2048,2816]{1,0:T(8,128)} fusion(bf16[2,1024,2816]{2,1,0:T(8,128)(2,1)} %param, bf16[1,2048,1024]{2,1,0:T(8,128)(2,1)} %param.2, f32[2048]{0:T(1024)S(1)} %add_rsqrt_fusion), kind=kOutput, calls=%fused_computation.79 | convolution fusion | flops 11817451520 | bytes 33038336 | tf_op jit(solution)/vmap(jvp())/dot_general | solution.py:20
  36.8 18.3 %fusion.65 = f32[2048,2816]{1,0:T(8,128)} fusion(bf16[2,1024,2816]{2,1,0:T(8,128)(2,1)} %param.3, bf16[1,2048,1024]{2,1,0:T(8,128)(2,1)S(1)} %copy-done.1, f32[2048]{0:T(1024)S(1)} %add_rsqrt_fusion), kind=kOutput, calls=%fused_computation.77 | convolution fusion | flops 11817451520 | bytes 33038336 | tf_op jit(solution)/vmap(jvp())/dot_general | solution.py:21
  55.1 19.6 %fusion.26 = bf16[2048,2816]{1,0:T(8,128)(2,1)} fusion(f32[2048,2816]{1,0:T(8,128)} %fusion.65, f32[2048,2816]{1,0:T(8,128)} %fusion.67), kind=kLoop, calls=%fused_computation.39 | loop fusion | flops 34603008 | bytes 57671680
  74.7 19.9 %fusion.39 = (f32[2048]{0:T(1024)S(1)}, bf16[1,1,2048,1024]{2,3,1,0:T(8,128)(2,1)}) fusion(bf16[2048,2816]{1,0:T(8,128)(2,1)} %fusion.26, bf16[2,2816,1024]{2,1,0:T(8,128)(2,1)} %param.4, bf16[1,2048,1024]{1,2,0:T(8,128)(2,1)} %copy), kind=kOutput, calls=%fused_computation.56 | convolution fusion | flops 11821643776 | bytes 25698304 | tf_op jit(solution)/vmap(jvp())/dot_general | solution.py:9
  94.7 0.6 copy-done.9
  95.2 20.2 %fusion.54 = f32[2048,2816]{1,0:T(8,128)} fusion(bf16[2,1024,2816]{2,1,0:T(8,128)(2,1)} %param, bf16[1,1,2048,1024]{2,3,1,0:T(8,128)(2,1)} %get-tuple-element.10, f32[2048]{0:T(1024)S(1)} %bitcast.337), kind=kOutput, calls=%fused_computation.66 | convolution fusion | flops 11817451520 | bytes 33038336 | tf_op jit(solution)/vmap(jvp())/dot_general | solution.py:20
  115.5 18.3 %fusion.58 = f32[2048,2816]{1,0:T(8,128)} fusion(bf16[2,1024,2816]{2,1,0:T(8,128)(2,1)} %param.3, bf16[1,1,2048,1024]{2,3,1,0:T(8,128)(2,1)S(1)} %copy-done.4, f32[2048]{0:T(1024)S(1)} %bitcast.338), kind=kOutput, calls=%fused_computation.70 | convolution fusion | flops 11817451520 | bytes 33038336 | tf_op jit(solution)/vmap(jvp())/dot_general | solution.py:21
  133.7 24.2 %fusion.48 = f32[1,2816,1024]{2,1,0:T(8,128)} fusion(f32[2048,2816]{1,0:T(8,128)} %fusion.58, f32[2048,2816]{1,0:T(8,128)} %fusion.54, bf16[1,2048,1024]{2,1,0:T(8,128)(2,1)S(1)} %copy-done.7), kind=kOutput, calls=%fused_computation.62 | convolution fusion | flops 11845763072 | bytes 61865984 | tf_op jit(solution)/vmap(transpose(jvp()))/dot_general | solution.py:9
  157.9 0.0 reduce-scatter.27.cloned.1.call-update
  157.9 0.0 reduce-scatter.29.cloned.1.call-start
  158.0 6.8 copy.1
  164.8 18.1 %convolution_convert_fusion.1 = bf16[2048,2816]{1,0:T(8,128)(2,1)} fusion(bf16[2,2816,1024]{2,1,0:T(8,128)(2,1)} %param.4, bf16[1,2048,1024]{2,1,0:T(8,128)(2,1)} %param.5), kind=kOutput, calls=%fused_computation.48 | convolution fusion | flops 11816927232 | bytes 21495808 | tf_op jit(solution)/vmap(transpose(jvp()))/dot_general | solution.py:9
  182.9 23.4 %fusion.6 = bf16[2048,2816]{1,0:T(8,128)(2,1)} fusion(f32[2048,2816]{1,0:T(8,128)} %fusion.54, f32[2048,2816]{1,0:T(8,128)} %fusion.58, bf16[2048,2816]{1,0:T(8,128)(2,1)} %convolution_convert_fusion.1), kind=kLoop, calls=%fused_computation.11 | loop fusion | flops 69206016 | bytes 69206016
  206.3 1.5 copy-done.3
  207.8 20.4 %fusion.24 = bf16[2048,1024]{0,1:T(8,128)(2,1)} fusion(bf16[2048,2816]{1,0:T(8,128)(2,1)S(1)} %copy-done.3, f32[2048,2816]{1,0:T(8,128)} %fusion.54, bf16[2,1024,2816]{2,1,0:T(8,128)(2,1)} %param.3), kind=kOutput, calls=%fused_computation.34 | convolution fusion | flops 11845763072 | bytes 44564480 | tf_op jit(solution)/vmap(transpose(jvp()))/dot_general | solution.py:21
  228.2 20.8 %fusion.41 = (f32[2048]{0:T(1024)S(1)}, bf16[2048,1024]{0,1:T(8,128)(2,1)}) fusion(bf16[1,1,2048,1024]{2,3,1,0:T(8,128)(2,1)} %get-tuple-element.10, bf16[2048,1024]{0,1:T(8,128)(2,1)} %fusion.24, bf16[2048,2816]{1,0:T(8,128)(2,1)} %fusion.6, bf16[2,1024,2816]{2,1,0:T(8,128)(2,1)} %param), kind=kOutput, calls=%fused_computation.58 | convolution fusion | flops 11821643776 | bytes 29892608 | tf_op jit(solution)/vmap(transpose(jvp()))/dot_general | solution.py:20
  249.1 4.7 fusion.81
  253.8 2.0 copy-done.6
  255.8 17.8 %convolution_bitcast_fusion = f32[1,2816,1024]{2,1,0:T(8,128)} fusion(bf16[2048,2816]{1,0:T(8,128)(2,1)} %fusion.26, bf16[2048,1024]{0,1:T(8,128)(2,1)S(1)} %fusion.81), kind=kOutput, calls=%fused_computation.63 | convolution fusion | flops 11811160064 | bytes 27262976 | tf_op jit(solution)/vmap(transpose(jvp()))/dot_general | solution.py:9
  273.6 0.0 reduce-scatter.29.cloned.1.call-update
  273.6 0.0 reduce-scatter.19.cloned.1.call-start
  273.6 18.9 %convolution_bitcast_fusion.1 = f32[1,1024,2816]{2,1,0:T(8,128)} fusion(bf16[2048,2816]{1,0:T(8,128)(2,1)} %fusion.6, bf16[1,1,2048,1024]{2,3,1,0:T(8,128)(2,1)} %get-tuple-element.10, f32[2048]{0:T(1024)S(1)} %bitcast.340), kind=kOutput, calls=%fused_computation.64 | convolution fusion | flops 11817451520 | bytes 27271168 | tf_op jit(solution)/vmap(transpose(jvp()))/dot_general | solution.py:20
  292.6 0.0 reduce-scatter.19.cloned.1.call-update
  292.6 0.0 reduce-scatter.21.cloned.1.call-start
  292.7 18.4 %convolution_convert_fusion = bf16[2048,2816]{1,0:T(8,128)(2,1)} fusion(bf16[2048,1024]{0,1:T(8,128)(2,1)} %copy-done.6, bf16[2,2816,1024]{2,1,0:T(8,128)(2,1)} %param.4), kind=kOutput, calls=%fused_computation.47 | convolution fusion | flops 11816927232 | bytes 21495808 | tf_op jit(solution)/vmap(transpose(jvp()))/dot_general | solution.py:9
  311.0 26.1 %fusion.51 = f32[1,1024,2816]{2,1,0:T(8,128)} fusion(f32[2048,2816]{1,0:T(8,128)} %fusion.67, f32[2048,2816]{1,0:T(8,128)} %fusion.65, bf16[2048,2816]{1,0:T(8,128)(2,1)} %convolution_convert_fusion, bf16[1,2048,1024]{1,2,0:T(8,128)(2,1)S(1)} %copy-done.8, f32[2048]{0:T(1024)S(1)} %copy-done.14), kind=kOutput, calls=%fused_computation.65 | convolution fusion | flops 11880890368 | bytes 73408512 | tf_op jit(solution)/vmap(transpose(jvp()))/dot_general | solution.py:20
  337.2 0.0 reduce-scatter.21.cloned.1.call-update
  337.2 0.0 reduce-scatter.23.cloned.1.call-start
  337.2 23.5 %fusion.42 = f32[1,1024,2816]{2,1,0:T(8,128)} fusion(bf16[2048,2816]{1,0:T(8,128)(2,1)} %convolution_convert_fusion.1, f32[2048,2816]{1,0:T(8,128)} %fusion.54, bf16[1,1,2048,1024]{2,3,1,0:T(8,128)(2,1)} %get-tuple-element.10, f32[2048]{0:T(1024)S(1)} %bitcast.341), kind=kOutput, calls=%fused_computation.60 | convolution fusion | flops 11852054528 | bytes 50339840 | tf_op jit(solution)/vmap(transpose(jvp()))/dot_general | solution.py:21
  360.8 0.0 reduce-scatter.23.cloned.1.call-update
  360.8 0.0 reduce-scatter.25.cloned.1.call-start
  360.9 23.7 %fusion.45 = f32[1,1024,2816]{2,1,0:T(8,128)} fusion(bf16[2048,2816]{1,0:T(8,128)(2,1)} %convolution_convert_fusion, f32[2048,2816]{1,0:T(8,128)} %fusion.67, bf16[1,2048,1024]{1,2,0:T(8,128)(2,1)} %copy, f32[2048]{0:T(1024)S(1)} %copy-done.14), kind=kOutput, calls=%fused_computation.61 | convolution fusion | flops 11852054528 | bytes 50339840 | tf_op jit(solution)/vmap(transpose(jvp()))/dot_general | solution.py:21
  384.5 0.0 all-gather.14.cloned.1.call-start
  384.6 0.6 copy-done.15
  385.2 0.6 dynamic-slice
  386.4 0.0 reduce-scatter.27.cloned.1.call-done
  386.4 1.5 convert_bitcast_fusion.4
  387.9 12.1 reduce-scatter.29.cloned.1.call-done
  400.0 1.5 convert_bitcast_fusion.3
  401.5 5.8 fusion.121
  407.3 0.0 all-gather.14.cloned.1.call-update
  407.3 0.0 all-gather.10.cloned.1.call-start
  407.4 112.8 %reduce-scatter.19.cloned.1.call-done = f32[1,128,2816]{2,1,0:T(8,128)} async-done(((f32[1,1024,2816]{2,1,0:T(8,128)}), f32[1,128,2816]{2,1,0:T(8,128)}) %reduce-scatter.19.cloned.1.call-update) | async-done | bytes 1441808
  520.1 1.4 convert_bitcast_fusion.8
  521.6 119.1 %reduce-scatter.21.cloned.1.call-done = f32[1,128,2816]{2,1,0:T(8,128)} async-done(((f32[1,1024,2816]{2,1,0:T(8,128)}), f32[1,128,2816]{2,1,0:T(8,128)}) %reduce-scatter.21.cloned.1.call-update) | async-done | bytes 1441808
  640.7 1.4 convert_bitcast_fusion.7
  642.1 5.8 fusion.123
  647.9 0.0 all-gather.12.cloned.1.call-start
  648.0 112.7 %reduce-scatter.23.cloned.1.call-done = f32[1,128,2816]{2,1,0:T(8,128)} async-done(((f32[1,1024,2816]{2,1,0:T(8,128)}), f32[1,128,2816]{2,1,0:T(8,128)}) %reduce-scatter.23.cloned.1.call-update) | async-done | bytes 1441808
  760.7 1.4 convert_bitcast_fusion.6
  762.1 119.1 %reduce-scatter.25.cloned.1.call-done = f32[1,128,2816]{2,1,0:T(8,128)} async-done(((f32[1,1024,2816]{2,1,0:T(8,128)}), f32[1,128,2816]{2,1,0:T(8,128)}) %reduce-scatter.25.cloned.1.call-update) | async-done | bytes 1441808
  881.3 1.4 convert_bitcast_fusion.5
  882.7 5.8 fusion.122
  888.5 100.7 %all-gather.14.cloned.1.call-done = bf16[1,2,2816,1024]{3,2,1,0:T(8,128)(2,1)} async-done(((bf16[1,2,352,1024]{3,2,1,0:T(8,128)(2,1)}), bf16[1,2,2816,1024]{3,2,1,0:T(8,128)(2,1)}) %all-gather.14.cloned.1.call-update) | async-done | bytes 11534352 | tf_op jit(solution)/reshape | solution.py:52
  989.2 108.6 %all-gather.10.cloned.1.call-done = bf16[1,2,1024,2816]{3,2,1,0:T(8,128)(2,1)} async-done(((bf16[1,2,128,2816]{3,2,1,0:T(8,128)(2,1)}), bf16[1,2,1024,2816]{3,2,1,0:T(8,128)(2,1)}) %all-gather.10.cloned.1.call-update) | async-done | bytes 11534352 | tf_op jit(solution)/reshape | solution.py:52
  1097.8 108.6 %all-gather.12.cloned.1.call-done = bf16[1,2,1024,2816]{3,2,1,0:T(8,128)(2,1)} async-done(((bf16[1,2,128,2816]{3,2,1,0:T(8,128)(2,1)}), bf16[1,2,1024,2816]{3,2,1,0:T(8,128)(2,1)}) %all-gather.12.cloned.1.call-update) | async-done | bytes 11534352 | tf_op jit(solution)/reshape | solution.py:52
  1206.4 11.7 copy.5
  1218.1 5.8 copy.6
  1223.9 0.8 slice-done.1
  1224.7 1.2 slice-done.2
  1225.9 4.4 copy.7
  (40 shorter events, 0.2 us)
Async XLA Ops:
  7.2 379.3 %reduce-scatter.27.cloned.1.call-start = ((), (), s32[]{:S(2)}) async-start(), calls=%async_computation.13 | async-start | bytes 12976128
  16.8 20.0 %copy-start.13 = (f32[2048]{0:T(1024)}, f32[2048]{0:T(1024)S(1)}, u32[]{:S(2)}) copy-start(f32[2048]{0:T(1024)S(1)} %add_rsqrt_fusion) | copy-start | bytes 24580
  16.8 20.0 %copy-start.1 = (bf16[1,2048,1024]{2,1,0:T(8,128)(2,1)S(1)}, bf16[1,2048,1024]{2,1,0:T(8,128)(2,1)}, u32[]{:S(2)}) copy-start(bf16[1,2048,1024]{2,1,0:T(8,128)(2,1)} %param.2) | copy-start | bytes 12582916
  94.6 0.6 copy-start.9
  94.6 20.8 %copy-start.11 = (f32[1,1,2048]{2,1,0:T(1,128)}, f32[1,1,2048]{2,1,0:T(1,128)S(1)}, u32[]{:S(2)}) copy-start(f32[1,1,2048]{2,1,0:T(1,128)S(1)} %rsqrt.31) | copy-start | bytes 24580
  95.2 20.2 %copy-start.4 = (bf16[1,1,2048,1024]{2,3,1,0:T(8,128)(2,1)S(1)}, bf16[1,1,2048,1024]{2,3,1,0:T(8,128)(2,1)}, u32[]{:S(2)}) copy-start(bf16[1,1,2048,1024]{2,3,1,0:T(8,128)(2,1)} %get-tuple-element.10) | copy-start | bytes 12582916
  115.5 18.3 %copy-start.7 = (bf16[1,2048,1024]{2,1,0:T(8,128)(2,1)S(1)}, bf16[1,2048,1024]{2,1,0:T(8,128)(2,1)}, u32[]{:S(2)}) copy-start(bf16[1,2048,1024]{2,1,0:T(8,128)(2,1)} %param.5) | copy-start | bytes 12582916
  157.9 242.1 %reduce-scatter.29.cloned.1.call-start = ((), (), s32[]{:S(2)}) async-start(), calls=%async_computation.14 | async-start | bytes 12976128
  182.9 24.9 %copy-start.3 = (bf16[2048,2816]{1,0:T(8,128)(2,1)S(1)}, bf16[2048,2816]{1,0:T(8,128)(2,1)}, u32[]{:S(2)}) copy-start(bf16[2048,2816]{1,0:T(8,128)(2,1)} %convolution_convert_fusion.1) | copy-start | bytes 34603012
  228.2 20.8 %copy-start.10 = (f32[2048]{0:T(1024)S(1)}, f32[2048]{0:T(1024)}, u32[]{:S(2)}) copy-start(f32[2048]{0:T(1024)} %copy-done.9) | copy-start | bytes 24580
  228.2 20.8 %copy-start = (bf16[1,2048,1024]{1,2,0:T(8,128)(2,1)S(1)}, bf16[1,2048,1024]{1,2,0:T(8,128)(2,1)}, u32[]{:S(2)}) copy-start(bf16[1,2048,1024]{1,2,0:T(8,128)(2,1)} %copy.1) | copy-start | bytes 12582916
  228.2 20.8 %copy-start.5 = (bf16[1,1,2048,1024]{2,3,1,0:T(8,128)(2,1)S(1)}, bf16[1,1,2048,1024]{2,3,1,0:T(8,128)(2,1)}, u32[]{:S(2)}) copy-start(bf16[1,1,2048,1024]{2,3,1,0:T(8,128)(2,1)} %get-tuple-element.10) | copy-start | bytes 12582916
  228.2 20.8 %copy-start.12 = (f32[1,1,2048]{2,1,0:T(1,128)S(1)}, f32[1,1,2048]{2,1,0:T(1,128)}, u32[]{:S(2)}) copy-start(f32[1,1,2048]{2,1,0:T(1,128)} %copy-done.11) | copy-start | bytes 24580
  253.8 2.0 copy-start.6
  273.6 246.6 %reduce-scatter.19.cloned.1.call-start = ((), (), s32[]{:S(2)}) async-start(), calls=%async_computation.9 | async-start | bytes 12976128
  292.6 18.4 %copy-start.14 = (f32[2048]{0:T(1024)S(1)}, f32[2048]{0:T(1024)}, u32[]{:S(2)}) copy-start(f32[2048]{0:T(1024)} %copy-done.13) | copy-start | bytes 24580
  292.6 348.1 %reduce-scatter.21.cloned.1.call-start = ((), (), s32[]{:S(2)}) async-start(), calls=%async_computation.10 | async-start | bytes 12976128
  292.7 18.4 %copy-start.8 = (bf16[1,2048,1024]{1,2,0:T(8,128)(2,1)S(1)}, bf16[1,2048,1024]{1,2,0:T(8,128)(2,1)}, u32[]{:S(2)}) copy-start(bf16[1,2048,1024]{1,2,0:T(8,128)(2,1)} %copy) | copy-start | bytes 12582916
  337.2 423.5 %reduce-scatter.23.cloned.1.call-start = ((), (), s32[]{:S(2)}) async-start(), calls=%async_computation.11 | async-start | bytes 12976128
  360.8 520.4 %reduce-scatter.25.cloned.1.call-start = ((), (), s32[]{:S(2)}) async-start(), calls=%async_computation.12 | async-start | bytes 12976128
  384.5 0.7 copy-start.15
  384.5 604.7 %all-gather.14.cloned.1.call-start = ((), (), s32[]{:S(2)}) async-start(), calls=%async_computation.8 | async-start | bytes 12976128 | tf_op jit(solution)/reshape | solution.py:52
  407.3 690.5 %all-gather.10.cloned.1.call-start = ((), (), s32[]{:S(2)}) async-start(), calls=%async_computation.6 | async-start | bytes 12976128 | tf_op jit(solution)/reshape | solution.py:52
  647.9 558.5 %all-gather.12.cloned.1.call-start = ((), (), s32[]{:S(2)}) async-start(), calls=%async_computation.7 | async-start | bytes 12976128 | tf_op jit(solution)/reshape | solution.py:52
  1206.4 11.7 copy-start.2
  1206.4 17.5 %slice-start = ((s8[11534336]{0:T(1024)(128)(4,1)}), s8[4194304]{0:T(1024)(128)(4,1)S(1)}, s32[]{:S(2)}) async-start(s8[11534336]{0:T(1024)(128)(4,1)} %bitcast.329), calls=%async_computation.15 | async-start | bytes 8388608
  1206.4 18.3 %slice-start.1 = ((s8[11534336]{0:T(1024)(128)(4,1)}), s8[4194304]{0:T(1024)(128)(4,1)S(1)}, s32[]{:S(2)}) async-start(s8[11534336]{0:T(1024)(128)(4,1)} %bitcast.329), calls=%async_computation.16 | async-start | bytes 8388608
  1218.1 7.9 slice-start.2
Sparse Core Ops, SparseCore 0:
  158.1 121.8 reduce-scatter.26
  282.2 117.7 reduce-scatter.28
  402.3 117.7 reduce-scatter.18
  522.9 117.7 reduce-scatter.20
  642.9 117.8 reduce-scatter.22
  763.4 117.7 reduce-scatter.24
  882.9 106.3 all-gather.13
  991.4 106.3 all-gather.9
  1100.0 106.3 all-gather.11
where the time goes:
time: 1240 us
  waiting for transfers between devices  794 us (64%)
  matrix products  309 us (25%)
  other arithmetic  76.9 us (6%)
  local copies, waits for them, and re-layouts  42.5 us (3%)
  between operations  15.1 us (1%)
    unnamed x15, waiting for transfers between devices  476 us
    reshape x3, waiting for transfers between devices, step(): t.reshape(-1, *t.shape[2:])  318 us
    dot_general x5, matrix products, layer(): gate = jnp.dot(a, w['w_gate'], preferred_element_type=jnp.float32)  106 us
    dot_general x5, matrix products, layer(): up = jnp.dot(a, w['w_up'], preferred_element_type=jnp.float32)  104 us
    dot_general x5, matrix products, matmul(): jnp.dot(a, w, preferred_element_type=jnp.float32).astype(jnp.bfloat16)  98.3 us
    unnamed x4, other arithmetic  47.8 us
    unnamed x43, local copies, waits for them, and re-layouts  41.9 us
  transfers between devices with their start and end apart: 9, of which 8 were waited for; matrix products, arithmetic and copies ran while one was open for 20% of the time, Pallas kernels for 0%

commit v1 on v0

v1 whole, which is shorter than its diff:
```python
import functools

import jax
import jax.numpy as jnp
from jax import lax
from jax.experimental import pallas as pl
from jax.experimental.pallas import tpu as pltpu
from jax.sharding import PartitionSpec as P

MESH = pl.DeviceIdType.MESH
BF, F32 = jnp.bfloat16, jnp.float32
CHIPS = 4
HOP = 2
SLOTS = 12
KEPT = 4
FAR = 1 + HOP * (CHIPS - 1)


def dot(a, b, dims):
    return lax.dot_general(a, b, (dims, ((), ())), preferred_element_type=F32)


def adamw(w, m, v, g):
    m = 0.9 * m + 0.1 * g
    v = 0.95 * v + 0.05 * g * g
    step = m * lax.rsqrt(v + 1e-8) + 0.1 * w
    return (w - 0.02 * step).astype(BF), m, v


def gates(gate, up, d_hidden):
    s = jax.nn.sigmoid(gate)
    gs = gate * s
    return (gs * up).astype(BF), (d_hidden * up * (s + gs * (1 - s))).astype(BF), (d_hidden * gs).astype(BF)


def kernel(dims, *refs):
    D, FF, T, C = dims
    (a2_ref, h1_ref, dy_ref, a1_ref, hid1_ref, gate1_ref, up1_ref, wg_ref, wu_ref, wd_ref) = refs[:10]
    m_refs, v_refs = refs[10:13], refs[13:16]
    wp_ref, mp_ref, vp_ref, hid2_ref, dg2_ref, du2_ref = refs[16:22]
    (A, B, E, acc, hid, dg, du, wgc, wuc, wdc, own, ex, R, L, mi, vi, wi, mo, vo, wo) = refs[22:42]
    (ex_s, ex_r, R_s, R_r, L_s, L_r, AR_s, AR_r, AL_s, AL_r, AD_s, AD_r) = refs[42:54]
    (big_sem, w_sem, row_sem, out_sem, in_sem, put_sem) = refs[54:]

    NC = FF // C
    Q = 6 * NC
    RB, RD, ND = D // 8, C // 8, D // C
    EVEN2, DOWN2, EVEN1, DOWN1 = 0, 2 * NC, 3 * NC, 5 * NC
    TT = min(T, 1024)

    me = lax.axis_index("dp")
    c, k = me // 2, me % 2
    partner, right, left = me + 1 - 2 * k, me + 2, me - 2

    barrier = pltpu.get_barrier_semaphore()
    for there, ok in ((partner, None), (right, c < CHIPS - 1), (left, c > 0)):
        def greet(there=there):
            pl.semaphore_signal(barrier, inc=1, device_id={"dp": there}, device_id_type=MESH)
        greet() if ok is None else pl.when(ok)(greet)

    def load(src, dst, sem):
        return pltpu.make_async_copy(src, dst, sem)

    def send(src, dst, s, r, there):
        return pltpu.make_async_remote_copy(src, dst, s, r, device_id={"dp": there}, device_id_type=MESH)

    def valid(q):
        return (q >= 0) & (q < Q)

    def ex_copy(q):
        s = q % SLOTS
        return send(own.at[s, 1 - k], ex.at[s], ex_s.at[s], ex_r.at[s], partner)

    def R_copy(q, b):
        s = q % SLOTS
        return send(R.at[s, b], R.at[s, b], R_s.at[s, b], R_r.at[s, b], right)

    def L_copy(q, b):
        s = q % SLOTS
        return send(L.at[s, b], L.at[s, b], L_s.at[s, b], L_r.at[s, b], left)

    def all_gather_copy(q, b, there, s_sem, r_sem):
        s, at = q % SLOTS, wp_ref.at[q, 2 * b + k]
        return send(at, at, s_sem.at[s, b], r_sem.at[s, b], there)

    def AR_copy(q, b):
        return all_gather_copy(q, b, right, AR_s, AR_r)

    def AL_copy(q, b):
        return all_gather_copy(q, b, left, AL_s, AL_r)

    def AD_copy(q, b):
        return all_gather_copy(q, b, partner, AD_s, AD_r)

    def pieces(q, whole, wide, do):
        layer = jnp.where(q < EVEN1, 1, 0)
        at = jnp.where(q < EVEN1, q, q - EVEN1)
        for which in (0, 1):
            @pl.when((at < DOWN2) & (at % 2 == which))
            def _():
                whole(which, layer, pl.multiple_of(at // 2 * C, C))
        @pl.when(at >= DOWN2)
        def _():
            wide(2, layer, pl.multiple_of((at - DOWN2) * RD, RD))

    def fetch(q, act):
        s = q % KEPT

        def whole(which, layer, column):
            cols = pl.ds(column, C)
            act(load(m_refs[which].at[layer, :, cols], mi.at[s], in_sem.at[s, 0, 0]))
            act(load(v_refs[which].at[layer, :, cols], vi.at[s], in_sem.at[s, 1, 0]))
            w = (wg_ref, wu_ref)[which]
            act(load(w.at[layer, pl.ds(pl.multiple_of(me * RB, RB), RB), cols], wi.at[s], in_sem.at[s, 2, 0]))

        def wide(which, layer, row):
            for p in range(ND):
                cols, to = pl.ds(p * C, C), pl.ds(p * RD, RD)
                act(load(m_refs[2].at[layer, pl.ds(row, RD), cols], mi.at[s, to], in_sem.at[s, 0, p]))
                act(load(v_refs[2].at[layer, pl.ds(row, RD), cols], vi.at[s, to], in_sem.at[s, 1, p]))
                rows = pl.ds(pl.multiple_of(me * (FF // 8) + row, RD), RD)
                act(load(wd_ref.at[layer, rows, cols], wi.at[s, to], in_sem.at[s, 2, p]))

        pieces(q, whole, wide, None)

    def puts(q):
        s = q % KEPT
        return (
            load(mo.at[s], mp_ref.at[q], put_sem.at[s, 0]),
            load(vo.at[s], vp_ref.at[q], put_sem.at[s, 1]),
            load(wo.at[s], wp_ref.at[q, me], put_sem.at[s, 2]),
        )

    def own_sends(q, act):
        s, n = q % KEPT, q % SLOTS
        to = wp_ref.at[q, me]

        @pl.when(c < CHIPS - 1)
        def _():
            act(send(wo.at[s], to, AR_s.at[n, c], AR_r.at[n, c], right))

        @pl.when(c > 0)
        def _():
            act(send(wo.at[s], to, AL_s.at[n, c], AL_r.at[n, c], left))

        act(send(wo.at[s], to, AD_s.at[n, c], AD_r.at[n, c], partner))

    def start(copy):
        copy.start()

    def wait(copy):
        copy.wait()

    def wait_send(copy):
        copy.wait_send()

    def service(t):
        @pl.when(valid(t - 1))
        def _():
            ex_copy(t - 1).wait_recv()

        q = t - 1 - HOP * c

        @pl.when(valid(q))
        def _():
            s = q % SLOTS
            for b in range(1, CHIPS):
                @pl.when((c > 0) & (b >= c))
                def _():
                    R_copy(q, b).wait_recv()
            for b in range(1, CHIPS):
                @pl.when((c > 0) & (b > c))
                def _():
                    R[s, b] = (own[s, k, b].astype(F32) + ex[s, b].astype(F32) + R[s, b].astype(F32)).astype(BF)

                @pl.when(c == 0)
                def _():
                    R[s, b] = (own[s, k, b].astype(F32) + ex[s, b].astype(F32)).astype(BF)

        p = t - 1 - HOP * (CHIPS - 1 - c)

        @pl.when(valid(p))
        def _():
            s = p % SLOTS
            for b in range(CHIPS - 1):
                @pl.when((c < CHIPS - 1) & (b <= c))
                def _():
                    L_copy(p, b).wait_recv()
            for b in range(CHIPS - 1):
                @pl.when((c < CHIPS - 1) & (b < c))
                def _():
                    L[s, b] = (own[s, k, b].astype(F32) + ex[s, b].astype(F32) + L[s, b].astype(F32)).astype(BF)

                @pl.when(c == CHIPS - 1)
                def _():
                    L[s, b] = (own[s, k, b].astype(F32) + ex[s, b].astype(F32)).astype(BF)

        @pl.when(valid(q))
        def _():
            for b in range(1, CHIPS):
                @pl.when(b > c)
                def _():
                    R_copy(q, b).start()

        @pl.when(valid(p))
        def _():
            for b in range(CHIPS - 1):
                @pl.when(b < c)
                def _():
                    L_copy(p, b).start()

        for b in range(CHIPS):
            q_r = t - FAR - HOP * (c - b)

            @pl.when((b < c) & valid(q_r))
            def _():
                AR_copy(q_r, b).wait_recv()
                @pl.when(c < CHIPS - 1)
                def _():
                    AR_copy(q_r, b).start()
                AD_copy(q_r, b).start()

            q_l = t - FAR - HOP * (b - c)

            @pl.when((b > c) & valid(q_l))
            def _():
                AL_copy(q_l, b).wait_recv()
                @pl.when(c > 0)
                def _():
                    AL_copy(q_l, b).start()
                AD_copy(q_l, b).start()

            far = jnp.abs(c - b)
            q_d = t - 1 - FAR - HOP * far

            @pl.when(valid(q_d))
            def _():
                AD_copy(q_d, b).wait_recv()

            q_s = t - 2 - FAR - HOP * far

            @pl.when(valid(q_s) & (b != c))
            def _():
                @pl.when((b < c) & (c < CHIPS - 1))
                def _():
                    AR_copy(q_s, b).wait_send()
                @pl.when((b > c) & (c > 0))
                def _():
                    AL_copy(q_s, b).wait_send()
                AD_copy(q_s, b).wait_send()

        q_e = t - FAR - 1

        @pl.when(valid(q_e))
        def _():
            ex_copy(q_e).wait_send()
            for b in range(CHIPS):
                if b > 0:
                    @pl.when(b > c)
                    def _():
                        R_copy(q_e, b).wait_send()
                if b < CHIPS - 1:
                    @pl.when(b < c)
                    def _():
                        L_copy(q_e, b).wait_send()

        q_o = t - FAR - 2

        @pl.when(valid(q_o))
        def _():
            for copy in puts(q_o):
                copy.wait()
            own_sends(q_o, wait_send)

        q_m = t - FAR + 2

        @pl.when(valid(q_m))
        def _():
            fetch(q_m, start)

        q_f = t - FAR

        @pl.when(valid(q_f))
        def _():
            fetch(q_f, wait)
            s, o = q_f % SLOTS, q_f % KEPT
            g = own[s, k, c].astype(F32) + ex[s, c].astype(F32) + R[s, c].astype(F32) + L[s, c].astype(F32)
            g = g.astype(BF).astype(F32)
            w, m, v = adamw(wi[o].astype(F32), mi[o], vi[o], g)
            wo[o], mo[o], vo[o] = w, m, v
            for copy in puts(q_f):
                copy.start()
            own_sends(q_f, start)

    def gate_loads(layer, j, act):
        s, at = j % 2, pl.ds(pl.multiple_of(j * C, C), C)
        act(load(wg_ref.at[layer, :, at], wgc.at[s], w_sem.at[s, 0]))
        act(load(wu_ref.at[layer, :, at], wuc.at[s], w_sem.at[s, 1]))

    def down_load(layer, j, act):
        s, at = j % 2, pl.ds(pl.multiple_of(j * C, C), C)
        act(load(wd_ref.at[layer, at, :], wdc.at[s], w_sem.at[s, 2]))

    def spills(j, act):
        s, at = j % 2, pl.ds(pl.multiple_of(j * C, C), C)
        act(load(hid.at[s], hid2_ref.at[at], out_sem.at[s, 0]))
        act(load(dg.at[s], dg2_ref.at[at], out_sem.at[s, 1]))
        act(load(du.at[s], du2_ref.at[at], out_sem.at[s, 2]))

    def row_loads(src, j, s, act):
        for d in range(8):
            rows = pl.ds(pl.multiple_of(d * (FF // 8) + j * RD, RD), RD)
            act(load(src.at[rows], hid.at[s, pl.ds(d * RD, RD)], row_sem.at[s, d]))

    def back_loads(j, s, act):
        at = pl.ds(pl.multiple_of(j * C, C), C)
        act(load(dg2_ref.at[at], dg.at[s], out_sem.at[s, 1]))
        act(load(du2_ref.at[at], du.at[s], out_sem.at[s, 2]))

    def gate1_loads(j, act):
        s, at = j % 2, pl.ds(pl.multiple_of(j * C, C), C)
        act(load(gate1_ref.at[at], acc.at[pl.ds(pl.multiple_of(s * 2 * C, C), C)], out_sem.at[s, 1]))
        act(load(up1_ref.at[at], acc.at[pl.ds(pl.multiple_of(s * 2 * C + C, C), C)], out_sem.at[s, 2]))

    def columns(i, size):
        return pl.ds(pl.multiple_of(i * size, size), size)

    def gate_gradient(t, a, d):
        s = t % SLOTS
        g = dot(a[...], d, ((1,), (1,))).astype(BF)
        for n in range(8):
            own[s, n % 2, n // 2] = g[n * RB : (n + 1) * RB]

    def down_gradient(t, rows, d):
        s = t % SLOTS

        @pl.loop(0, ND)
        def _(p):
            g = dot(rows, d[columns(p, C), :], ((1,), (1,))).astype(BF)
            for n in range(8):
                own[s, n % 2, n // 2, columns(p, RD), :] = g[n * RD : (n + 1) * RD]

    def produce(t):
        phase2 = t < EVEN1
        at = jnp.where(phase2, t, t - EVEN1)
        j = at // 2
        s = j % 2
        gate_even = (at < DOWN2) & (at % 2 == 0)
        gate_odd = (at < DOWN2) & (at % 2 == 1)

        @pl.when(phase2 & gate_even)
        def _():
            @pl.when(j == 0)
            def _():
                for i, (ref, to) in enumerate(((a2_ref, A), (dy_ref, B))):
                    load(ref, to, big_sem.at[i]).wait()
            gate_loads(1, j, wait)
            down_load(1, j, wait)

            @pl.when(j + 1 < NC)
            def _():
                gate_loads(1, j + 1, start)
                down_load(1, j + 1, start)

            @pl.when(j >= 2)
            def _():
                spills(j - 2, wait)

            @pl.loop(0, T // TT)
            def _(i):
                x = A[:, columns(i, TT)]
                gate = dot(wgc[s], x, ((0,), (0,)))
                up = dot(wuc[s], x, ((0,), (0,)))
                d_hidden = dot(wdc[s], B[:, columns(i, TT)], ((1,), (0,))).astype(BF).astype(F32)
                hid[s, :, columns(i, TT)], dg[s, :, columns(i, TT)], du[s, :, columns(i, TT)] = gates(gate, up, d_hidden)

            spills(j, start)
            gate_gradient(t, A, dg[s])

        @pl.when(phase2 & gate_odd)
        def _():
            gate_gradient(t, A, du[s])

            @pl.when(j == NC - 1)
            def _():
                spills(NC - 2, wait)
                spills(NC - 1, wait)
                gate_loads(1, 0, start)
                back_loads(0, NC % 2, start)
                row_loads(hid2_ref, 0, NC % 2, start)
                load(h1_ref, E, big_sem.at[2]).start()

        @pl.when(phase2 & (at >= DOWN2))
        def _():
            i = at - DOWN2
            n, other = (i + NC) % 2, (i + NC + 1) % 2
            gate_loads(1, i, wait)
            back_loads(i, n, wait)
            row_loads(hid2_ref, i, n, wait)

            @pl.when(i + 1 < NC)
            def _():
                gate_loads(1, i + 1, start)
                back_loads(i + 1, other, start)
                row_loads(hid2_ref, i + 1, other, start)

            down_gradient(t, hid[n], B)

            @pl.loop(0, T // TT)
            def _(x):
                cols = columns(x, TT)
                new = dot(wgc[i % 2], dg[n, :, cols], ((1,), (0,))) + dot(wuc[i % 2], du[n, :, cols], ((1,), (0,)))

                @pl.when(i == 0)
                def _():
                    acc[:, cols] = new

                @pl.when(i > 0)
                def _():
                    acc[:, cols] += new

            @pl.when(i == NC - 1)
            def _():
                load(h1_ref, E, big_sem.at[2]).wait()
                down_load(0, 0, start)
                TS = min(T, 128)

                @pl.loop(0, T // TS)
                def _(x):
                    cols = columns(x, TS)
                    h = E[:, cols].astype(F32)
                    da = acc[:, cols].astype(BF).astype(F32)
                    scale = lax.rsqrt(jnp.mean(h * h, 0, keepdims=True) + 1e-6)
                    inner = jnp.mean(da * h, 0, keepdims=True)
                    dh = (da * scale - h * (scale * scale * scale * inner)).astype(BF).astype(F32)
                    A[:, cols] = (B[:, cols].astype(F32) + dh).astype(BF)

                gate1_loads(0, start)
                load(a1_ref, E, big_sem.at[2]).start()

        @pl.when(~phase2 & gate_even)
        def _():
            down_load(0, j, wait)
            gate1_loads(j, wait)

            @pl.when(j + 1 < NC)
            def _():
                down_load(0, j + 1, start)
                gate1_loads(j + 1, start)

            @pl.loop(0, T // TT)
            def _(i):
                cols = columns(i, TT)
                gate, up = acc[columns(2 * s, C), cols], acc[columns(2 * s + 1, C), cols]
                d_hidden = dot(wdc[s], A[:, cols], ((1,), (0,))).astype(BF).astype(F32)
                _, dg[s, :, cols], du[s, :, cols] = gates(gate, up, d_hidden)

            @pl.when(j == 0)
            def _():
                load(a1_ref, E, big_sem.at[2]).wait()

            gate_gradient(t, E, dg[s])

        @pl.when(~phase2 & gate_odd)
        def _():
            @pl.when(j == NC - 1)
            def _():
                row_loads(hid1_ref, 0, 0, start)

            gate_gradient(t, E, du[s])

        @pl.when(~phase2 & (at >= DOWN2))
        def _():
            i = at - DOWN2
            row_loads(hid1_ref, i, i % 2, wait)

            @pl.when(i + 1 < NC)
            def _():
                row_loads(hid1_ref, i + 1, (i + 1) % 2, start)

            down_gradient(t, hid[i % 2], A)

    for i, (ref, to) in enumerate(((a2_ref, A), (dy_ref, B))):
        load(ref, to, big_sem.at[i]).start()
    gate_loads(1, 0, start)
    down_load(1, 0, start)

    @pl.when(c == 0)
    def _():
        R[:, 0] = jnp.zeros((SLOTS, RB, C), BF)

    @pl.when(c == CHIPS - 1)
    def _():
        L[:, CHIPS - 1] = jnp.zeros((SLOTS, RB, C), BF)

    pl.semaphore_wait(barrier, 1 + jnp.where(c > 0, 1, 0) + jnp.where(c < CHIPS - 1, 1, 0))

    @pl.loop(0, Q + 3 + 2 * HOP * (CHIPS - 1))
    def _(t):
        service(t)

        @pl.when(t < Q)
        def _():
            produce(t)
            ex_copy(t).start()


def mega(dims, *arrays):
    D, FF, T, C = dims
    Q, RB, RD, ND = 6 * (FF // C), D // 8, C // 8, D // C
    hbm = pl.BlockSpec(memory_space=pltpu.HBM)
    dma = lambda *shape: pltpu.SemaphoreType.DMA(shape)
    return pl.pallas_call(
        functools.partial(kernel, dims),
        out_shape=(
            jax.ShapeDtypeStruct((Q, 8, RB, C), BF),
            jax.ShapeDtypeStruct((Q, RB, C), F32),
            jax.ShapeDtypeStruct((Q, RB, C), F32),
        )
        + (jax.ShapeDtypeStruct((FF, T), BF),) * 3,
        in_specs=[hbm] * 16,
        out_specs=(hbm,) * 6,
        scratch_shapes=[pltpu.VMEM((D, T), BF)] * 3
        + [pltpu.VMEM((D, T), F32)]
        + [pltpu.VMEM((2, C, T), BF)] * 3
        + [pltpu.VMEM((2, D, C), BF)] * 2
        + [pltpu.VMEM((2, C, D), BF)]
        + [pltpu.VMEM((SLOTS, 2, CHIPS, RB, C), BF)]
        + [pltpu.VMEM((SLOTS, CHIPS, RB, C), BF)] * 3
        + [pltpu.VMEM((KEPT, RB, C), F32)] * 2
        + [pltpu.VMEM((KEPT, RB, C), BF)]
        + [pltpu.VMEM((KEPT, RB, C), F32)] * 2
        + [pltpu.VMEM((KEPT, RB, C), BF)]
        + [dma(SLOTS)] * 2
        + [dma(SLOTS, CHIPS)] * 10
        + [dma(3), dma(2, 3), dma(2, 8), dma(2, 3), dma(KEPT, 3, ND), dma(KEPT, 3)],
        compiler_params=pltpu.CompilerParams(collective_id=0, has_side_effects=True, vmem_limit_bytes=63 * 2**20),
        name="step",
    )(*arrays)[:3]


def place_kernel(dims, wg, wu, wd, mg, mu, md, vg, vu, vd, *outs):
    D, FF, T, C = dims
    RD, ND = C // 8, D // C
    for src, dst in ((wg, outs[0]), (wu, outs[1])):
        dst[...] = src[...].reshape(dst.shape)
    for src, dst in zip((mg, mu, vg, vu), (outs[3], outs[4], outs[6], outs[7])):
        dst[...] = src[...]
    for p in range(ND):
        rows, cols = slice(p * RD, (p + 1) * RD), slice(p * C, (p + 1) * C)
        outs[2][0, :, :, cols] = wd[0, :, rows]
        outs[5][0, :, cols] = md[0, rows]
        outs[8][0, :, cols] = vd[0, rows]


def place(dims, wp, mp, vp):
    D, FF, T, C = dims
    NC, RB, RD = FF // C, D // 8, C // 8
    first = lambda n: 3 * NC * (1 - n)
    chunk = (lambda n, j: first(n) + 2 * j, lambda n, j: first(n) + 2 * j + 1, lambda n, j: first(n) + 2 * NC + j)
    w_in = [pl.BlockSpec((1, 8, RB, C), lambda n, j, f=f: (f(n, j), 0, 0, 0)) for f in chunk]
    m_in = [pl.BlockSpec((1, RB, C), lambda n, j, f=f: (f(n, j), 0, 0)) for f in chunk]
    wide = lambda rows: pl.BlockSpec((1, rows, C), lambda n, j: (n, 0, j))
    w_out = [wide(D)] * 2 + [pl.BlockSpec((1, 8, RD, D), lambda n, j: (n, 0, j, 0))]
    m_out = [wide(RB)] * 2 + [pl.BlockSpec((1, RD, D), lambda n, j: (n, j, 0))]
    m_shapes = [jax.ShapeDtypeStruct((2, RB, FF), F32)] * 2 + [jax.ShapeDtypeStruct((2, FF // 8, D), F32)]
    outs = pl.pallas_call(
        functools.partial(place_kernel, dims),
        grid=(2, NC),
        in_specs=w_in + m_in + m_in,
        out_specs=w_out + m_out + m_out,
        out_shape=[jax.ShapeDtypeStruct((2, D, FF), BF)] * 2
        + [jax.ShapeDtypeStruct((2, 8, FF // 8, D), BF)]
        + m_shapes
        + m_shapes,
        compiler_params=pltpu.CompilerParams(vmem_limit_bytes=48 * 2**20),
        name="place",
    )(wp, wp, wp, mp, mp, mp, vp, vp, vp)
    outs = list(outs)
    outs[2] = outs[2].reshape(2, FF, D)
    return tuple(outs)


def solution(mesh):
    def local(x, dy, wg, wu, wd, mg, mu, md, vg, vu, vd):
        T, D = x.shape[1:]
        FF = wg.shape[2]
        dims = (D, FF, T, 256 if FF % 256 == 0 else 128)
        h0, dy = x[0].T, dy[0].T

        def normed(h):
            wide = h.astype(F32)
            return (wide * lax.rsqrt(jnp.mean(wide * wide, 0, keepdims=True) + 1e-6)).astype(BF)

        a1 = normed(h0)
        gate1 = dot(wg[0], a1, ((0,), (0,)))
        up1 = dot(wu[0], a1, ((0,), (0,)))
        hid1 = (jax.nn.silu(gate1) * up1).astype(BF)
        h1 = h0 + dot(wd[0], hid1, ((0,), (0,))).astype(BF)
        a2 = normed(h1)
        packed = mega(dims, a2, h1, dy, a1, hid1, gate1, up1, wg, wu, wd, mg, mu, md, vg, vu, vd)
        return place(dims, *packed)

    whole, rows, mine = P(None, None, None), P(None, "dp", None), P(("rep", "dp"), None, None)
    out_whole, out_rows = P("rep", None, None), P("rep", "dp", None)
    return jax.shard_map(
        local,
        mesh=mesh,
        in_specs=(mine, mine) + (whole,) * 3 + (rows,) * 6,
        out_specs=(out_whole,) * 3 + (out_rows,) * 6,
        check_vma=False,
    )
```

time: 1240 us -> 583 us (0.47)
  waiting for transfers between devices: 794 us -> 0 us
  Pallas kernels: 0 us -> 490 us
  matrix products: 309 us -> 65.1 us
  other arithmetic: 76.9 us -> 12 us
  local copies, waits for them, and re-layouts: 42.5 us -> 14.9 us
  between operations: 15.1 us -> 0.85 us
    pallas_call x0 -> x2, Pallas kernels: none -> 490 us  [the longest x1 450 us: mega(): pl.pallas_call(functools.partial(kernel, dims), out_shape=(jax.ShapeDtype...]
    unnamed x15 -> x0, waiting for transfers between devices: 476 us -> none
    reshape x3 -> x0, waiting for transfers between devices: 318 us -> none  [step(): t.reshape(-1, *t.shape[2:])]
    dot_general x15 -> x3, matrix products: 309 us -> 65.1 us  [dot(): return lax.dot_general(a, b, (dims, ((), ())), preferred_element_type=F32)]
    unnamed x4 -> x0, other arithmetic: 47.8 us -> none
    unnamed x43 -> x6, local copies, waits for them, and re-layouts: 41.9 us -> 14.9 us
    reshape x3 -> x0, other arithmetic: 17.3 us -> none  [step(): t.reshape(-1, *t.shape[2:])]
  transfers between devices with their start and end apart: 9 -> 0, of which waited for: 8 -> 0; matrix products, arithmetic and copies ran while one was open for 20% -> 0% of each run, Pallas kernels for 0% -> 0%
where the time goes in v1:
time: 583 us; the launch traced here: 582 us
  Pallas kernels  490 us (84%)
  matrix products  65.1 us (11%)
  local copies, waits for them, and re-layouts  14.9 us (3%)
  other arithmetic  12 us (2%)
    pallas_call x1, Pallas kernels, mega(): pl.pallas_call(functools.partial(kernel, dims), out_shape=(jax.ShapeDtype...  450 us
    dot_general x3, matrix products, dot(): return lax.dot_general(a, b, (dims, ((), ())), preferred_element_type=F32)  65.1 us
    pallas_call x1, Pallas kernels, place(): pl.pallas_call(functools.partial(place_kernel, dims), grid=(2, NC), in_sp...  39.6 us
    unnamed x6, local copies, waits for them, and re-layouts  14.9 us

profile of v1, /device:TPU:0, one launch (start us, length us, event | category | flops | bytes accessed | tf_op | source)
XLA Modules:
  0.0 582.4 jit_solution(13077961165330728357)
XLA Ops:
  0.6 6.4 %copy.20 = bf16[1,2048,1024]{1,2,0:T(8,128)(2,1)} copy(bf16[1,2048,1024]{2,1,0:T(8,128)(2,1)} %param.11) | data formatting | bytes 8388608 | tf_op args[0]
  7.1 3.1 fusion
  10.2 5.6 fusion.14.refs_3_
  15.7 6.5 %copy.23 = bf16[1,2048,1024]{1,2,0:T(8,128)(2,1)} copy(bf16[1,2048,1024]{2,1,0:T(8,128)(2,1)} %param.12) | data formatting | bytes 8388608 | tf_op args[1]
  22.2 0.0 copy-start
  22.2 20.3 %convolution_bitcast_fusion.1.refs_5_ = f32[2816,2048]{1,0:T(8,128)} fusion(bf16[2,1024,2816]{2,1,0:T(8,128)(2,1)} %refs_7_.1, bf16[1,2048,1024]{1,2,0:T(8,128)(2,1)} %copy.20, f32[2048]{0:T(1024)S(1)} %add_rsqrt_fusion.1), kind=kOutput, calls=%fused_computation.2 | convolution fusion | flops 11817451520 | bytes 33038336 | tf_op jit(solution)/shard_map/dot_general | solution.py:20
  42.5 0.0 copy-done
  42.6 27.2 %multiply_convert_fusion = (bf16[2816,2048]{1,0:T(8,128)(2,1)}, f32[2816,2048]{1,0:T(8,128)}) fusion(f32[2816,2048]{1,0:T(8,128)} %convolution_bitcast_fusion.1.refs_5_, bf16[2,1024,2816]{2,1,0:T(8,128)(2,1)} %refs_8_.1, bf16[1,2048,1024]{1,2,0:T(8,128)(2,1)S(1)} %copy-done, f32[2048]{0:T(1024)S(1)} %add_rsqrt_fusion.1), kind=kOutput, calls=%fused_computation | convolution fusion | flops 11852054528 | bytes 67641344 | tf_op jit(solution)/shard_map/dot_general | solution.py:20
  69.7 17.6 %fusion.2 = (f32[2048]{0:T(1024)S(1)}, bf16[1024,2048]{1,0:T(8,128)(2,1)S(1)}) fusion(bf16[2816,2048]{1,0:T(8,128)(2,1)} %get-tuple-element.33.refs_4_, bf16[2,2816,1024]{2,1,0:T(8,128)(2,1)} %refs_9_.1, bf16[1,2048,1024]{1,2,0:T(8,128)(2,1)S(1)} %copy-done), kind=kOutput, calls=%fused_computation.9 | convolution fusion | flops 11821643776 | bytes 25698304 | tf_op jit(solution)/shard_map/dot_general | solution.py:20
  87.3 0.0 copy-start.1
  87.4 2.0 copy-done.1
  89.4 3.4 fusion.3.refs_0_
  92.7 449.9 %step.1 = (bf16[66,8,128,256]{3,2,1,0:T(8,128)(2,1)}, f32[66,128,256]{2,1,0:T(8,128)}, f32[66,128,256]{2,1,0:T(8,128)}, bf16[2816,2048]{1,0:T(8,128)(2,1)}, bf16...) custom-call(bf16[1024,2048]{1,0:T(8,128)(2,1)} %fusion.3.refs_0_, bf16[1024,2048]{1,0:T(8,128)(2,1)} %copy-done.1, ...), custom_call_target="tpu_custom_call" | custom-call | tf_op jit(solution)/shard_map/step/pallas_call | solution.py:513
  542.7 39.6 %place.1 = (bf16[2,1024,2816]{2,1,0:T(8,128)(2,1)}, bf16[2,1024,2816]{2,1,0:T(8,128)(2,1)}, bf16[2,8,352,1024]{3,2,1,0:T(8,128)(2,1)}, f32[2,128,2816]{2,1,0:T(8...) custom-call(bf16[66,8,128,256]{3,2,1,0:T(8,128)(2,1)} %get-tuple-ele, ...), custom_call_target="tpu_custom_call" | custom-call | tf_op jit(solution)/shard_map/place/pallas_call | solution.py:567
  (2 shorter events, 0.0 us)
Async XLA Ops:
  22.2 20.3 %copy-start = (bf16[1,2048,1024]{1,2,0:T(8,128)(2,1)S(1)}, bf16[1,2048,1024]{1,2,0:T(8,128)(2,1)}, u32[]{:S(2)}) copy-start(bf16[1,2048,1024]{1,2,0:T(8,128)(2,1)} %copy.20) | copy-start | bytes 12582916
  87.3 2.0 copy-start.1

commit v2 on v0

v2 whole, which is shorter than its diff:
```python
import functools

import jax
import jax.numpy as jnp
from jax import lax
from jax.experimental import pallas as pl
from jax.experimental.pallas import tpu as pltpu
from jax.sharding import PartitionSpec as P

MESH = pl.DeviceIdType.MESH
BF, F32 = jnp.bfloat16, jnp.float32
CHIPS = 4
FIRST = 1
HOP = 1
SPREAD = 2
SLOTS = 11
ROWS = 2
RING = 16
KEPT = 3


def dot(a, b, dims):
    return lax.dot_general(a, b, (dims, ((), ())), preferred_element_type=F32)


def adamw(w, m, v, g):
    m = 0.9 * m + 0.1 * g
    v = 0.95 * v + 0.05 * g * g
    step = m * lax.rsqrt(v + 1e-8) + 0.1 * w
    return (w - 0.02 * step).astype(BF), m, v


def gates(gate, up, d_hidden):
    s = jax.nn.sigmoid(gate)
    gs = gate * s
    return (gs * up).astype(BF), (d_hidden * up * (s + gs * (1 - s))).astype(BF), (d_hidden * gs).astype(BF)


def kernel(dims, *refs):
    D, FF, T, C = dims
    x_ref, dy_ref, wg_ref, wu_ref, wd_ref = refs[:5]
    m_refs, v_refs = refs[5:8], refs[8:11]
    wp_ref, mp_ref, vp_ref, hid2_ref, dg2_ref, du2_ref = refs[11:17]
    (AT, BT, acc, rows, hid, dg, du, wgc, wuc, wdc, own, ex, R, L, mi, vi, wi, mo, vo, wo) = refs[17:37]
    (ex_s, ex_r, R_s, R_r, L_s, L_r, AR_s, AR_r, AL_s, AL_r, AD_s, AD_r) = refs[37:49]
    (w_sem, row_sem, out_sem, in_sem, put_sem, x_sem) = refs[49:]

    NC = FF // C
    Q = 6 * NC
    RB, RD, ND = D // 8, C // 8, D // C
    PAIRS = (NC + 1) // 2
    assert PAIRS + 4 <= NC
    DOWN, HALF = 2 * NC, 3 * NC
    TT = T // 2
    TR, TS = min(T, 256), min(TT, 256)
    later = pl.ds(TT, TT)
    parts = [slice(n * C, (n + 1) * C) for n in range(ND)]

    me = lax.axis_index("dp")
    c, k = me // 2, me % 2
    partner, right, left = me + 1 - 2 * k, me + 2, me - 2

    barrier = pltpu.get_barrier_semaphore()
    for there, ok in ((partner, None), (right, c < CHIPS - 1), (left, c > 0)):
        def greet(there=there):
            pl.semaphore_signal(barrier, inc=1, device_id={"dp": there}, device_id_type=MESH)
        greet() if ok is None else pl.when(ok)(greet)

    def load(src, dst, sem):
        return pltpu.make_async_copy(src, dst, sem)

    def send(src, dst, s, r, there):
        return pltpu.make_async_remote_copy(src, dst, s, r, device_id={"dp": there}, device_id_type=MESH)

    def chunk(t):
        return t, (t >= 0) & (t < Q)

    def end(b):
        return FIRST + HOP * jnp.maximum(b, CHIPS - 1 - b)

    def ex_copy(q):
        s = q % SLOTS
        return send(own.at[s, 1 - k], ex.at[s], ex_s.at[s], ex_r.at[s], partner)

    def R_copy(q, b):
        s = q % SLOTS
        return send(R.at[s, b], R.at[s, b], R_s.at[s, b], R_r.at[s, b], right)

    def L_copy(q, b):
        s = q % SLOTS
        return send(L.at[s, b], L.at[s, b], L_s.at[s, b], L_r.at[s, b], left)

    def all_gather_copy(q, b, there, s_sem, r_sem):
        s, at = q % SLOTS, wp_ref.at[q, 2 * b + k]
        return send(at, at, s_sem.at[s, b], r_sem.at[s, b], there)

    def AR_copy(q, b):
        return all_gather_copy(q, b, right, AR_s, AR_r)

    def AL_copy(q, b):
        return all_gather_copy(q, b, left, AL_s, AL_r)

    def AD_copy(q, b):
        return all_gather_copy(q, b, partner, AD_s, AD_r)

    def pieces(q, whole, wide):
        layer = jnp.where(q < HALF, 1, 0)
        at = jnp.where(q < HALF, q, q - HALF)
        for which in (0, 1):
            @pl.when((at < DOWN) & (at % 2 == which))
            def _():
                whole(which, layer, pl.multiple_of(at // 2 * C, C))
        @pl.when(at >= DOWN)
        def _():
            wide(2, layer, pl.multiple_of((at - DOWN) * RD, RD))

    def fetch(q, act):
        s = q % KEPT

        def whole(which, layer, column):
            cols = pl.ds(column, C)
            act(load(m_refs[which].at[layer, :, cols], mi.at[s], in_sem.at[s, 0, 0]))
            act(load(v_refs[which].at[layer, :, cols], vi.at[s], in_sem.at[s, 1, 0]))
            w = (wg_ref, wu_ref)[which]
            act(load(w.at[layer, pl.ds(pl.multiple_of(me * RB, RB), RB), cols], wi.at[s], in_sem.at[s, 2, 0]))

        def wide(which, layer, row):
            for p in range(ND):
                cols, to = pl.ds(p * C, C), pl.ds(p * RD, RD)
                act(load(m_refs[2].at[layer, pl.ds(row, RD), cols], mi.at[s, to], in_sem.at[s, 0, p]))
                act(load(v_refs[2].at[layer, pl.ds(row, RD), cols], vi.at[s, to], in_sem.at[s, 1, p]))
                rows = pl.ds(pl.multiple_of(me * (FF // 8) + row, RD), RD)
                act(load(wd_ref.at[layer, rows, cols], wi.at[s, to], in_sem.at[s, 2, p]))

        pieces(q, whole, wide)

    def puts(q):
        s = q % KEPT
        return (
            load(mo.at[s], mp_ref.at[q], put_sem.at[s, 0]),
            load(vo.at[s], vp_ref.at[q], put_sem.at[s, 1]),
            load(wo.at[s], wp_ref.at[q, me], put_sem.at[s, 2]),
        )

    def own_sends(q, act):
        s, n = q % KEPT, q % SLOTS
        to = wp_ref.at[q, me]

        @pl.when(c < CHIPS - 1)
        def _():
            act(send(wo.at[s], to, AR_s.at[n, c], AR_r.at[n, c], right))

        @pl.when(c > 0)
        def _():
            act(send(wo.at[s], to, AL_s.at[n, c], AL_r.at[n, c], left))

        act(send(wo.at[s], to, AD_s.at[n, c], AD_r.at[n, c], partner))

    def start(copy):
        copy.start()

    def wait(copy):
        copy.wait()

    def wait_send(copy):
        copy.wait_send()

    def service(t):
        new, is_new = chunk(t - FIRST)

        @pl.when(is_new)
        def _():
            ex_copy(new).wait_recv()

        q, is_q = chunk(t - FIRST - HOP * c)
        p, is_p = chunk(t - FIRST - HOP * (CHIPS - 1 - c))

        def up_sum(b):
            s = q % SLOTS
            terms = own[s, k, b].astype(F32) + ex[s, b].astype(F32)

            @pl.when(c == 0)
            def _():
                R[s, b] = terms.astype(BF)

            @pl.when(c > 0)
            def _():
                R_copy(q, b).wait_recv()
                R[s, b] = (terms + R[s, b].astype(F32)).astype(BF)

        def down_sum(b):
            s = p % SLOTS
            terms = own[s, k, b].astype(F32) + ex[s, b].astype(F32)

            @pl.when(c == CHIPS - 1)
            def _():
                L[s, b] = terms.astype(BF)

            @pl.when(c < CHIPS - 1)
            def _():
                L_copy(p, b).wait_recv()
                L[s, b] = (terms + L[s, b].astype(F32)).astype(BF)

        for n in range(CHIPS - 1):
            b = CHIPS - 1 - n
            go_up, go_down = is_q & (b > c), is_p & (n < c)

            @pl.when(go_up)
            def _():
                up_sum(b)

            @pl.when(go_down)
            def _():
                down_sum(n)

            @pl.when(go_up)
            def _():
                R_copy(q, b).start()

            @pl.when(go_down)
            def _():
                L_copy(p, n).start()

        q_e, gone_e = chunk(t - FIRST - HOP * (CHIPS - 1) - 2)

        @pl.when(gone_e)
        def _():
            ex_copy(q_e).wait_send()
            for b in range(CHIPS):
                if b > 0:
                    @pl.when(b > c)
                    def _():
                        R_copy(q_e, b).wait_send()
                if b < CHIPS - 1:
                    @pl.when(b < c)
                    def _():
                        L_copy(q_e, b).wait_send()

        q_o, gone_o = chunk(t - end(c) - 3)

        @pl.when(gone_o)
        def _():
            for copy in puts(q_o):
                copy.wait()
            own_sends(q_o, wait_send)

        q_m, ahead = chunk(t - end(c) + 2)

        @pl.when(ahead)
        def _():
            fetch(q_m, start)

        q_f, whole = chunk(t - end(c))

        @pl.when(whole)
        def _():
            @pl.when(c > 0)
            def _():
                R_copy(q_f, c).wait_recv()

            @pl.when(c < CHIPS - 1)
            def _():
                L_copy(q_f, c).wait_recv()

            fetch(q_f, wait)
            s, o = q_f % SLOTS, q_f % KEPT
            g = own[s, k, c].astype(F32) + ex[s, c].astype(F32) + R[s, c].astype(F32) + L[s, c].astype(F32)
            g = g.astype(BF).astype(F32)
            w, m, v = adamw(wi[o].astype(F32), mi[o], vi[o], g)
            wo[o], mo[o], vo[o] = w, m, v
            for copy in puts(q_f):
                copy.start()
            own_sends(q_f, start)

        for b in range(CHIPS):
            far = end(b) + SPREAD * jnp.abs(c - b)
            q_r, arrived = chunk(t - far)

            @pl.when((b < c) & arrived)
            def _():
                AR_copy(q_r, b).wait_recv()
                @pl.when(c < CHIPS - 1)
                def _():
                    AR_copy(q_r, b).start()
                AD_copy(q_r, b).start()

            @pl.when((b > c) & arrived)
            def _():
                AL_copy(q_r, b).wait_recv()
                @pl.when(c > 0)
                def _():
                    AL_copy(q_r, b).start()
                AD_copy(q_r, b).start()

            q_d, over = chunk(t - far - 1)

            @pl.when(over)
            def _():
                AD_copy(q_d, b).wait_recv()

            q_s, gone = chunk(t - far - 3)

            @pl.when(gone & (b != c))
            def _():
                @pl.when((b < c) & (c < CHIPS - 1))
                def _():
                    AR_copy(q_s, b).wait_send()
                @pl.when((b > c) & (c > 0))
                def _():
                    AL_copy(q_s, b).wait_send()
                AD_copy(q_s, b).wait_send()

    def chunk_of(j):
        return pl.ds(pl.multiple_of(j * C, C), C)

    def columns(i, size):
        return pl.ds(pl.multiple_of(i * size, size), size)

    def gate_loads(layer, j, n, act):
        act(load(wg_ref.at[layer, :, chunk_of(j)], wgc.at[n % 2], w_sem.at[n % 2, 0]))
        act(load(wu_ref.at[layer, :, chunk_of(j)], wuc.at[n % 2], w_sem.at[n % 2, 1]))

    def down_load(layer, j, n, act):
        act(load(wd_ref.at[layer, chunk_of(j), :], wdc.at[n % 2], w_sem.at[n % 2, 2]))

    def spills(j, act):
        s, at = j % 2, chunk_of(j)
        act(load(hid.at[s], hid2_ref.at[at], out_sem.at[s, 0]))
        act(load(dg.at[s, :, later], dg2_ref.at[at], out_sem.at[s, 1]))
        act(load(du.at[s, :, later], du2_ref.at[at], out_sem.at[s, 2]))

    def row_loads(i, act):
        for d in range(8):
            at = pl.ds(pl.multiple_of(d * (FF // 8) + i * RD, RD), RD)
            act(load(hid2_ref.at[at], hid.at[1 + i % 2, pl.ds(d * RD, RD)], row_sem.at[i % 2, d]))

    def back_loads(i, act):
        act(load(dg2_ref.at[chunk_of(i)], dg.at[i % 2, :, later], out_sem.at[i % 2, 1]))
        act(load(du2_ref.at[chunk_of(i)], du.at[i % 2, :, later], out_sem.at[i % 2, 2]))

    def token_load(ref, i, act):
        act(load(ref.at[columns(i, TR)], rows.at[i % ROWS], x_sem.at[i % ROWS]))

    def forward():
        NT = T // TR
        for i in range(min(ROWS, NT)):
            token_load(x_ref, i, start)
        gate_loads(0, 0, 0, start)
        down_load(0, 0, 0, start)

        @pl.loop(0, NT)
        def _(i):
            cols = columns(i, TR)
            token_load(x_ref, i, wait)
            total = jnp.zeros((1, TR), F32)
            for part in parts:
                h = rows[i % ROWS, :, part].T
                AT[1, part, cols] = h
                total += jnp.sum(h.astype(F32) ** 2, 0, keepdims=True)
            scale = lax.rsqrt(total / D + 1e-6)
            for part in parts:
                AT[0, part, cols] = (AT[1, part, cols].astype(F32) * scale).astype(BF)

            @pl.when(i + ROWS < NT)
            def _():
                token_load(x_ref, i + ROWS, start)

        for i in range(min(ROWS, NT)):
            token_load(dy_ref, i, start)

        @pl.loop(0, NC)
        def _(j):
            s = j % 2
            gate_loads(0, j, j, wait)
            down_load(0, j, j, wait)

            @pl.when(j + 1 < NC)
            def _():
                gate_loads(0, j + 1, j + 1, start)
                down_load(0, j + 1, j + 1, start)

            @pl.when(j + 1 == NC)
            def _():
                gate_loads(1, 0, NC, start)
                down_load(1, 0, NC, start)

            @pl.when(j < NT)
            def _():
                token_load(dy_ref, j, wait)

            tile = jnp.minimum(j, NT - 1)
            for part in parts:
                BT[1, part, columns(tile, TR)] = rows[tile % ROWS, :, part].T
            gate = dot(wgc[s], AT[0], ((0,), (0,)))
            up = dot(wuc[s], AT[0], ((0,), (0,)))
            hid[s] = (gate * jax.nn.sigmoid(gate) * up).astype(BF)

            @pl.loop(0, T // TT)
            def _(i):
                cols = columns(i, TT)
                acc[:, cols] = jnp.where(j > 0, acc[:, cols], 0.0) + dot(wdc[s], hid[s, :, cols], ((0,), (0,)))

            @pl.when(j + ROWS < NT)
            def _():
                token_load(dy_ref, j + ROWS, start)

        @pl.loop(0, T // TS)
        def _(i):
            cols = columns(i, TS)
            total = jnp.zeros((1, TS), F32)
            for part in parts:
                h = (AT[1, part, cols].astype(F32) + acc[part, cols].astype(BF).astype(F32)).astype(BF)
                BT[0, part, cols] = h
                total += jnp.sum(h.astype(F32) ** 2, 0, keepdims=True)
            scale = lax.rsqrt(total / D + 1e-6)
            for part in parts:
                AT[1, part, cols] = (BT[0, part, cols].astype(F32) * scale).astype(BF)

    def make_gates(layer, j, n, first, last):
        s = j % 2

        @pl.when(first == 0)
        def _():
            gate_loads(layer, j, n, wait)
            down_load(layer, j, n, wait)

            @pl.when(j + 1 < NC)
            def _():
                gate_loads(layer, j + 1, n + 1, start)
                down_load(layer, j + 1, n + 1, start)

            @pl.when(j >= 2)
            def _():
                spills(j - 2, wait)

        @pl.loop(first, last)
        def _(i):
            cols = columns(i, TT)
            gate = dot(wgc[n % 2], AT[layer, :, cols], ((0,), (0,)))
            up = dot(wuc[n % 2], AT[layer, :, cols], ((0,), (0,)))
            d_hidden = dot(wdc[n % 2], BT[layer, :, cols], ((1,), (0,))).astype(BF).astype(F32)
            hid[s, :, cols], dg[s, :, cols], du[s, :, cols] = gates(gate, up, d_hidden)

        @pl.when(last == 2)
        def _():
            spills(j, start)

    def into_normed(i, n, half):
        cols = columns(half, TT)
        from_gate = dot(wgc[n % 2], dg[i % 2, :, cols], ((1,), (0,)))
        from_up = dot(wuc[n % 2], du[i % 2, :, cols], ((1,), (0,)))
        acc[:, cols] = jnp.where(i > 0, acc[:, cols], 0.0) + (from_gate + from_up)

    def into_layer_1(half):
        @pl.loop(0, TT // TS)
        def _(i):
            cols = columns(half * (TT // TS) + i, TS)
            square, inner = jnp.zeros((1, TS), F32), jnp.zeros((1, TS), F32)
            for part in parts:
                h, da = BT[0, part, cols].astype(F32), acc[part, cols].astype(BF).astype(F32)
                square += jnp.sum(h * h, 0, keepdims=True)
                inner += jnp.sum(da * h, 0, keepdims=True)
            scale = lax.rsqrt(square / D + 1e-6)
            pull = scale * scale * scale * (inner / D)
            for part in parts:
                h, da = BT[0, part, cols].astype(F32), acc[part, cols].astype(BF).astype(F32)
                dh = (da * scale - h * pull).astype(BF).astype(F32)
                BT[0, part, cols] = (BT[1, part, cols].astype(F32) + dh).astype(BF)

    def produce(t):
        second = t < HALF
        layer = jnp.where(second, 1, 0)
        at = jnp.where(second, t, t - HALF)
        j, i = at // 2, at - DOWN

        @pl.when((at < DOWN) & (at % 2 == 0))
        def _():
            for n, d in ((0, dg), (1, du)):
                g = dot(AT[layer], d[j % 2], ((1,), (1,))).astype(BF)
                for e in range(8):
                    own[(t + n) % SLOTS, e % 2, e // 2] = g[e * RB : (e + 1) * RB]
            ex_copy(t).start()
            ex_copy(t + 1).start()

            @pl.when(second)
            def _():
                into_normed(j, NC + j, 0)

        @pl.when((at < DOWN) & (at % 2 == 1))
        def _():
            @pl.when(j + 1 < NC)
            def _():
                make_gates(layer, j + 1, jnp.where(second, NC, 3 * NC) + j + 1, 0, 2)

            @pl.when(j + 1 == NC)
            def _():
                if NC > 1:
                    spills(NC - 2, wait)
                spills(NC - 1, wait)
                row_loads(0, start)

                @pl.when(second)
                def _():
                    for n in range(2):
                        gate_loads(1, n, n, start)
                        back_loads(n, start)

        @pl.when(at >= DOWN)
        def _():
            row_loads(i, wait)

            @pl.when(i + 1 < NC)
            def _():
                row_loads(i + 1, start)

            g = dot(hid[1 + i % 2], BT[layer], ((1,), (1,))).astype(BF)
            for p in range(ND):
                for e in range(8):
                    own[t % SLOTS, e % 2, e // 2, p * RD : (p + 1) * RD] = g[e * RD : (e + 1) * RD, p * C : (p + 1) * C]
            ex_copy(t).start()

        @pl.when((at >= DOWN) & second & (i < PAIRS))
        def _():
            for n in range(2):
                @pl.when(2 * i + n < NC)
                def _():
                    gate_loads(1, 2 * i + n, n, wait)
                    back_loads(2 * i + n, wait)
                    into_normed(2 * i + n, n, 1)

                @pl.when(2 * i + n + 2 < NC)
                def _():
                    gate_loads(1, 2 * i + n + 2, n, start)
                    back_loads(2 * i + n + 2, start)

        @pl.when((at >= DOWN) & second & (i >= PAIRS) & (i < PAIRS + 2))
        def _():
            @pl.when(i == PAIRS)
            def _():
                gate_loads(0, 0, 3 * NC, start)
                down_load(0, 0, 3 * NC, start)

            into_layer_1(i - PAIRS)

        @pl.when((at >= DOWN) & second & (i >= PAIRS + 2) & (i < PAIRS + 4))
        def _():
            make_gates(0, 0, 3 * NC, i - PAIRS - 2, i - PAIRS - 1)

    @pl.when(c == 0)
    def _():
        R[:, 0] = jnp.zeros((SLOTS, RB, C), BF)

    @pl.when(c == CHIPS - 1)
    def _():
        L[:, CHIPS - 1] = jnp.zeros((SLOTS, RB, C), BF)

    forward()
    make_gates(1, 0, NC, 0, 2)
    pl.semaphore_wait(barrier, 1 + jnp.where(c > 0, 1, 0) + jnp.where(c < CHIPS - 1, 1, 0))

    @pl.loop(0, Q + FIRST + (HOP + SPREAD) * (CHIPS - 1) + 3)
    def _(t):
        service(t)

        @pl.when(t < Q)
        def _():
            produce(t)


def mega(dims, *arrays):
    D, FF, T, C = dims
    Q, RB, RD, ND = 6 * (FF // C), D // 8, C // 8, D // C
    hbm = pl.BlockSpec(memory_space=pltpu.HBM)
    dma = lambda *shape: pltpu.SemaphoreType.DMA(shape)
    return pl.pallas_call(
        functools.partial(kernel, dims),
        out_shape=(
            jax.ShapeDtypeStruct((Q, 8, RB, C), BF),
            jax.ShapeDtypeStruct((Q, RB, C), F32),
            jax.ShapeDtypeStruct((Q, RB, C), F32),
        )
        + (jax.ShapeDtypeStruct((FF, T), BF),)
        + (jax.ShapeDtypeStruct((FF, T // 2), BF),) * 2,
        in_specs=[hbm] * 11,
        out_specs=(hbm,) * 6,
        scratch_shapes=[pltpu.VMEM((2, D, T), BF)] * 2
        + [pltpu.VMEM((D, T), F32)]
        + [pltpu.VMEM((ROWS, min(T, 256), D), BF)]
        + [pltpu.VMEM((3, C, T), BF)]
        + [pltpu.VMEM((2, C, T), BF)] * 2
        + [pltpu.VMEM((2, D, C), BF)] * 2
        + [pltpu.VMEM((2, C, D), BF)]
        + [pltpu.VMEM((SLOTS, 2, CHIPS, RB, C), BF)]
        + [pltpu.VMEM((SLOTS, CHIPS, RB, C), BF)] * 3
        + [pltpu.VMEM((KEPT, RB, C), F32)] * 2
        + [pltpu.VMEM((KEPT, RB, C), BF)]
        + [pltpu.VMEM((KEPT, RB, C), F32)] * 2
        + [pltpu.VMEM((KEPT, RB, C), BF)]
        + [dma(SLOTS)] * 2
        + [dma(SLOTS, CHIPS)] * 10
        + [dma(2, 3), dma(2, 8), dma(2, 3), dma(KEPT, 3, ND), dma(KEPT, 3), dma(ROWS)],
        compiler_params=pltpu.CompilerParams(collective_id=0, has_side_effects=True, vmem_limit_bytes=67043328),
        name="step",
    )(*arrays)[:3]


def place_kernel(dims, *refs):
    D, FF, T, C = dims
    NC, RB, RD, ND = FF // C, D // 8, C // 8, D // C
    Q, HALF, DOWN = 6 * NC, 3 * NC, 2 * NC
    ins, outs, bufs, (in_sem, out_sem) = refs[:3], refs[3:12], refs[12:15], refs[15:]
    RING, LAG = bufs[0].shape[0], bufs[0].shape[0] // 2

    def copy_in(q, n):
        return pltpu.make_async_copy(ins[n].at[q], bufs[n].at[q % RING], in_sem.at[q % RING, n])

    def copies_out(q, act):
        layer = jnp.where(q < HALF, 1, 0)
        at = jnp.where(q < HALF, q, q - HALF)
        s = q % RING
        cols = pl.ds(pl.multiple_of(at // 2 * C, C), C)
        rows = pl.ds(pl.multiple_of((at - DOWN) * RD, RD), RD)
        for which in range(2):
            @pl.when((at < DOWN) & (at % 2 == which))
            def _():
                for n in range(3):
                    to = outs[3 * n + which]
                    to = to.at[layer, :, :, cols] if n == 0 else to.at[layer, :, cols]
                    act(pltpu.make_async_copy(bufs[n].at[s], to, out_sem.at[s, n, 0]))

        @pl.when(at >= DOWN)
        def _():
            for n in range(3):
                for p in range(ND):
                    piece, part = pl.ds(p * RD, RD), pl.ds(p * C, C)
                    if n == 0:
                        src, to = bufs[0].at[s, :, piece], outs[2].at[layer, :, rows, part]
                    else:
                        src, to = bufs[n].at[s, piece], outs[3 * n + 2].at[layer, rows, part]
                    act(pltpu.make_async_copy(src, to, out_sem.at[s, n, p]))

    @pl.loop(0, Q + RING)
    def _(q):
        @pl.when(q >= RING)
        def _():
            copies_out(q - RING, lambda copy: copy.wait())

        @pl.when(q < Q)
        def _():
            for n in range(3):
                copy_in(q, n).start()

        @pl.when((q >= LAG) & (q < Q + LAG))
        def _():
            for n in range(3):
                copy_in(q - LAG, n).wait()
            copies_out(q - LAG, lambda copy: copy.start())


def place(dims, wp, mp, vp):
    D, FF, T, C = dims
    RB, RD, ND = D // 8, C // 8, D // C
    hbm = pl.BlockSpec(memory_space=pltpu.HBM)
    states = [jax.ShapeDtypeStruct((2, RB, FF), F32)] * 2 + [jax.ShapeDtypeStruct((2, FF // 8, D), F32)]
    outs = pl.pallas_call(
        functools.partial(place_kernel, dims),
        in_specs=[hbm] * 3,
        out_specs=[hbm] * 9,
        out_shape=[jax.ShapeDtypeStruct((2, 8, RB, FF), BF)] * 2
        + [jax.ShapeDtypeStruct((2, 8, FF // 8, D), BF)]
        + states
        + states,
        scratch_shapes=[pltpu.VMEM((RING, 8, RB, C), BF)]
        + [pltpu.VMEM((RING, RB, C), F32)] * 2
        + [pltpu.SemaphoreType.DMA((RING, 3)), pltpu.SemaphoreType.DMA((RING, 3, ND))],
        compiler_params=pltpu.CompilerParams(vmem_limit_bytes=48 * 2**20),
        name="place",
    )(wp, mp, vp)
    return tuple(t.reshape(2, -1, t.shape[-1]) for t in outs)


def solution(mesh):
    def local(x, dy, wg, wu, wd, mg, mu, md, vg, vu, vd):
        T, D = x.shape[1:]
        FF = wg.shape[2]
        dims = (D, FF, T, 256 if FF % 256 == 0 else 128)
        return place(dims, *mega(dims, x[0], dy[0], wg, wu, wd, mg, mu, md, vg, vu, vd))

    whole, rows, mine = P(None, None, None), P(None, "dp", None), P(("rep", "dp"), None, None)
    out_whole, out_rows = P("rep", None, None), P("rep", "dp", None)
    return jax.shard_map(
        local,
        mesh=mesh,
        in_specs=(mine, mine) + (whole,) * 3 + (rows,) * 6,
        out_specs=(out_whole,) * 3 + (out_rows,) * 6,
        check_vma=False,
    )
```

time: 1240 us -> 499 us (0.40)
  waiting for transfers between devices: 794 us -> 0 us
  Pallas kernels: 0 us -> 498 us
  matrix products: 309 us -> 0 us
  other arithmetic: 76.9 us -> 0 us
  local copies, waits for them, and re-layouts: 42.5 us -> 0 us
  between operations: 15.1 us -> 0.81 us
    pallas_call x0 -> x2, Pallas kernels: none -> 498 us  [the longest x1 463 us: mega(): pl.pallas_call(functools.partial(kernel, dims), out_shape=(jax.ShapeDtype...]
    unnamed x15 -> x0, waiting for transfers between devices: 476 us -> none
    reshape x3 -> x0, waiting for transfers between devices: 318 us -> none  [step(): t.reshape(-1, *t.shape[2:])]
    dot_general x15 -> x0, matrix products: 309 us -> none  [the longest x5 106 us: layer(): gate = jnp.dot(a, w['w_gate'], preferred_element_type=jnp.float32)]
    unnamed x4 -> x0, other arithmetic: 47.8 us -> none
    unnamed x43 -> x0, local copies, waits for them, and re-layouts: 41.9 us -> none
    reshape x3 -> x0, other arithmetic: 17.3 us -> none  [step(): t.reshape(-1, *t.shape[2:])]
  transfers between devices with their start and end apart: 9 -> 0, of which waited for: 8 -> 0; matrix products, arithmetic and copies ran while one was open for 20% -> 0% of each run, Pallas kernels for 0% -> 0%
where the time goes in v2:
time: 499 us
  Pallas kernels  498 us (100%)
    pallas_call x1, Pallas kernels, mega(): pl.pallas_call(functools.partial(kernel, dims), out_shape=(jax.ShapeDtype...  463 us
    pallas_call x1, Pallas kernels, place(): pl.pallas_call(functools.partial(place_kernel, dims), in_specs=[hbm] * 3,...  35.2 us

profile of v2, /device:TPU:0, one launch (start us, length us, event | category | flops | bytes accessed | tf_op | source)
XLA Modules:
  0.0 499.1 jit_solution(1190985504788158837)
XLA Ops:
  0.6 463.1 %step.1 = (bf16[66,8,128,256]{3,2,1,0:T(8,128)(2,1)}, f32[66,128,256]{2,1,0:T(8,128)}, f32[66,128,256]{2,1,0:T(8,128)}, bf16[2816,2048]{1,0:T(8,128)(2,1)}, bf16...) custom-call(bf16[2048,1024]{1,0:T(8,128)(2,1)} %bitcast.5, bf16[2048,1024]{1,0:T(8,128)(2,1)} %bitcast.6, ...), custom_call_target="tpu_custom_call" | custom-call | tf_op jit(solution)/shard_map/step/pallas_call | solution.py:575
  463.7 35.2 %place.1 = (bf16[2,8,128,2816]{3,2,1,0:T(8,128)(2,1)}, bf16[2,8,128,2816]{3,2,1,0:T(8,128)(2,1)}, bf16[2,8,352,1024]{3,2,1,0:T(8,128)(2,1)}, f32[2,128,2816]{2,1...) custom-call(bf16[66,8,128,256]{3,2,1,0:T(8,128)(2,1)} %get-tuple-ele, ...), custom_call_target="tpu_custom_call" | custom-call | tf_op jit(solution)/shard_map/place/pallas_call | solution.py:665

commit v3 on v2

--- a/solution.py
+++ b/solution.py
@@ -13,8 +13,8 @@
 FIRST = 1
 HOP = 1
 SPREAD = 2
-SLOTS = 11
-ROWS = 2
+SLOTS = 10
+ROWS = 4
 RING = 16
 KEPT = 3
 
@@ -41,18 +41,18 @@
     x_ref, dy_ref, wg_ref, wu_ref, wd_ref = refs[:5]
     m_refs, v_refs = refs[5:8], refs[8:11]
     wp_ref, mp_ref, vp_ref, hid2_ref, dg2_ref, du2_ref = refs[11:17]
-    (AT, BT, acc, rows, hid, dg, du, wgc, wuc, wdc, own, ex, R, L, mi, vi, wi, mo, vo, wo) = refs[17:37]
-    (ex_s, ex_r, R_s, R_r, L_s, L_r, AR_s, AR_r, AL_s, AL_r, AD_s, AD_r) = refs[37:49]
-    (w_sem, row_sem, out_sem, in_sem, put_sem, x_sem) = refs[49:]
+    (AT, B, H, acc, rows, hid, dg, du, wgc, wuc, wdc, own, ex, R, L, mi, vi, wi, mo, vo, wo) = refs[17:38]
+    (ex_s, ex_r, R_s, R_r, L_s, L_r, AR_s, AR_r, AL_s, AL_r, AD_s, AD_r) = refs[38:50]
+    (w_sem, row_sem, out_sem, in_sem, put_sem, x_sem, dy_sem) = refs[50:]
 
     NC = FF // C
     Q = 6 * NC
     RB, RD, ND = D // 8, C // 8, D // C
     PAIRS = (NC + 1) // 2
-    assert PAIRS + 4 <= NC
+    assert PAIRS + 3 <= NC
     DOWN, HALF = 2 * NC, 3 * NC
     TT = T // 2
-    TR, TS = min(T, 256), min(TT, 256)
+    TR, TS = min(T // 4, 256), min(TT, 256)
     later = pl.ds(TT, TT)
     parts = [slice(n * C, (n + 1) * C) for n in range(ND)]
 
@@ -338,112 +338,101 @@
         act(load(dg2_ref.at[chunk_of(i)], dg.at[i % 2, :, later], out_sem.at[i % 2, 1]))
         act(load(du2_ref.at[chunk_of(i)], du.at[i % 2, :, later], out_sem.at[i % 2, 2]))
 
-    def token_load(ref, i, act):
-        act(load(ref.at[columns(i, TR)], rows.at[i % ROWS], x_sem.at[i % ROWS]))
+    def token_load(i, act):
+        act(load(x_ref.at[columns(i, TR)], rows.at[i % ROWS], x_sem.at[i % ROWS]))
 
     def forward():
-        NT = T // TR
-        for i in range(min(ROWS, NT)):
-            token_load(x_ref, i, start)
-        gate_loads(0, 0, 0, start)
-        down_load(0, 0, 0, start)
-
-        @pl.loop(0, NT)
-        def _(i):
-            cols = columns(i, TR)
-            token_load(x_ref, i, wait)
-            total = jnp.zeros((1, TR), F32)
-            for part in parts:
-                h = rows[i % ROWS, :, part].T
-                AT[1, part, cols] = h
-                total += jnp.sum(h.astype(F32) ** 2, 0, keepdims=True)
-            scale = lax.rsqrt(total / D + 1e-6)
-            for part in parts:
-                AT[0, part, cols] = (AT[1, part, cols].astype(F32) * scale).astype(BF)
-
-            @pl.when(i + ROWS < NT)
-            def _():
-                token_load(x_ref, i + ROWS, start)
-
-        for i in range(min(ROWS, NT)):
-            token_load(dy_ref, i, start)
-
-        @pl.loop(0, NC)
+        quarters = range(4)
+        TQ = T // 4
+
+        def take_in(n):
+            for i in range(n * (TQ // TR), (n + 1) * (TQ // TR)):
+                cols = slice(i * TR, (i + 1) * TR)
+                token_load(i, wait)
+                total = jnp.zeros((1, TR), F32)
+                for part in parts:
+                    h = rows[i % ROWS, :, part].T
+                    AT[1, part, cols] = h
+                    total += jnp.sum(h.astype(F32) ** 2, 0, keepdims=True)
+                scale = lax.rsqrt(total / D + 1e-6)
+                for part in parts:
+                    AT[0, part, cols] = (AT[1, part, cols].astype(F32) * scale).astype(BF)
+                if i + ROWS < T // TR:
+                    token_load(i + ROWS, start)
+
+        def hidden(j, n):
+            now = slice(n * TQ, (n + 1) * TQ)
+            gate = dot(wgc[j % 2], AT[0, :, now], ((0,), (0,)))
+            up = dot(wuc[j % 2], AT[0, :, now], ((0,), (0,)))
+            hid[0, :, now] = (gate * jax.nn.sigmoid(gate) * up).astype(BF)
+
+        def add(j, n):
+            now = slice(n * TQ, (n + 1) * TQ)
+            acc[:, now] = jnp.where(j > 0, acc[:, now], 0.0) + dot(wdc[j % 2], hid[0, :, now], ((0,), (0,)))
+
+        def leave(n):
+            for i in range(n * (TQ // TR), (n + 1) * (TQ // TR)):
+                cols = slice(i * TR, (i + 1) * TR)
+                total = jnp.zeros((1, TR), F32)
+                for part in parts:
+                    h = AT[1, part, cols] + acc[part, cols].astype(BF)
+                    H[part, cols] = h
+                    total += jnp.sum(h.astype(F32) ** 2, 0, keepdims=True)
+                scale = lax.rsqrt(total / D + 1e-6)
+                for part in parts:
+                    AT[1, part, cols] = (H[part, cols].astype(F32) * scale).astype(BF)
+
+        def staggered(steps):
+            for n in range(4 + len(steps) - 1):
+                for behind, step in enumerate(steps):
+                    if n - behind in quarters:
+                        step(n - behind)
+
+        def weights(j, act):
+            gate_loads(0, j, j, act)
+            down_load(0, j, j, act)
+
+        for i in range(min(ROWS, T // TR)):
+            token_load(i, start)
+        weights(0, start)
+        load(dy_ref, B.at[1], dy_sem).start()
+        weights(0, wait)
+        weights(1, start)
+        staggered((take_in, functools.partial(hidden, 0), functools.partial(add, 0)))
+
+        @pl.loop(1, NC - 1)
         def _(j):
-            s = j % 2
-            gate_loads(0, j, j, wait)
-            down_load(0, j, j, wait)
-
-            @pl.when(j + 1 < NC)
-            def _():
-                gate_loads(0, j + 1, j + 1, start)
-                down_load(0, j + 1, j + 1, start)
-
-            @pl.when(j + 1 == NC)
-            def _():
-                gate_loads(1, 0, NC, start)
-                down_load(1, 0, NC, start)
-
-            @pl.when(j < NT)
-            def _():
-                token_load(dy_ref, j, wait)
-
-            tile = jnp.minimum(j, NT - 1)
-            for part in parts:
-                BT[1, part, columns(tile, TR)] = rows[tile % ROWS, :, part].T
-            gate = dot(wgc[s], AT[0], ((0,), (0,)))
-            up = dot(wuc[s], AT[0], ((0,), (0,)))
-            hid[s] = (gate * jax.nn.sigmoid(gate) * up).astype(BF)
-
-            @pl.loop(0, T // TT)
-            def _(i):
-                cols = columns(i, TT)
-                acc[:, cols] = jnp.where(j > 0, acc[:, cols], 0.0) + dot(wdc[s], hid[s, :, cols], ((0,), (0,)))
-
-            @pl.when(j + ROWS < NT)
-            def _():
-                token_load(dy_ref, j + ROWS, start)
-
-        @pl.loop(0, T // TS)
-        def _(i):
-            cols = columns(i, TS)
-            total = jnp.zeros((1, TS), F32)
-            for part in parts:
-                h = (AT[1, part, cols].astype(F32) + acc[part, cols].astype(BF).astype(F32)).astype(BF)
-                BT[0, part, cols] = h
-                total += jnp.sum(h.astype(F32) ** 2, 0, keepdims=True)
-            scale = lax.rsqrt(total / D + 1e-6)
-            for part in parts:
-                AT[1, part, cols] = (BT[0, part, cols].astype(F32) * scale).astype(BF)
-
-    def make_gates(layer, j, n, first, last):
+            weights(j, wait)
+            weights(j + 1, start)
+            staggered((functools.partial(hidden, j), functools.partial(add, j)))
+
+        weights(NC - 1, wait)
+        gate_loads(1, 0, NC, start)
+        down_load(1, 0, NC, start)
+        staggered((functools.partial(hidden, NC - 1), functools.partial(add, NC - 1), leave))
+
+    def make_gates(layer, j, n):
         s = j % 2
-
-        @pl.when(first == 0)
-        def _():
-            gate_loads(layer, j, n, wait)
-            down_load(layer, j, n, wait)
-
-            @pl.when(j + 1 < NC)
-            def _():
-                gate_loads(layer, j + 1, n + 1, start)
-                down_load(layer, j + 1, n + 1, start)
-
-            @pl.when(j >= 2)
-            def _():
-                spills(j - 2, wait)
-
-        @pl.loop(first, last)
-        def _(i):
-            cols = columns(i, TT)
+        gate_loads(layer, j, n, wait)
+        down_load(layer, j, n, wait)
+
+        @pl.when(j + 1 < NC)
+        def _():
+            gate_loads(layer, j + 1, n + 1, start)
+            down_load(layer, j + 1, n + 1, start)
+
+        @pl.when(j >= 2)
+        def _():
+            spills(j - 2, wait)
+
+        for i in range(2):
+            cols = pl.ds(i * TT, TT)
             gate = dot(wgc[n % 2], AT[layer, :, cols], ((0,), (0,)))
             up = dot(wuc[n % 2], AT[layer, :, cols], ((0,), (0,)))
-            d_hidden = dot(wdc[n % 2], BT[layer, :, cols], ((1,), (0,))).astype(BF).astype(F32)
+            d_hidden = dot(wdc[n % 2], B[layer, cols, :], ((1,), (1,))).astype(BF).astype(F32)
             hid[s, :, cols], dg[s, :, cols], du[s, :, cols] = gates(gate, up, d_hidden)
 
-        @pl.when(last == 2)
-        def _():
-            spills(j, start)
+        spills(j, start)
 
     def into_normed(i, n, half):
         cols = columns(half, TT)
@@ -457,15 +446,14 @@
             cols = columns(half * (TT // TS) + i, TS)
             square, inner = jnp.zeros((1, TS), F32), jnp.zeros((1, TS), F32)
             for part in parts:
-                h, da = BT[0, part, cols].astype(F32), acc[part, cols].astype(BF).astype(F32)
+                h, da = H[part, cols].astype(F32), acc[part, cols].astype(BF).astype(F32)
                 square += jnp.sum(h * h, 0, keepdims=True)
                 inner += jnp.sum(da * h, 0, keepdims=True)
             scale = lax.rsqrt(square / D + 1e-6)
             pull = scale * scale * scale * (inner / D)
             for part in parts:
-                h, da = BT[0, part, cols].astype(F32), acc[part, cols].astype(BF).astype(F32)
-                dh = (da * scale - h * pull).astype(BF).astype(F32)
-                BT[0, part, cols] = (BT[1, part, cols].astype(F32) + dh).astype(BF)
+                h, da = H[part, cols].astype(F32), acc[part, cols].astype(BF).astype(F32)
+                B[0, cols, part] = B[1, cols, part] + (da * scale - h * pull).astype(BF).T
 
     def produce(t):
         second = t < HALF
@@ -488,10 +476,6 @@
 
         @pl.when((at < DOWN) & (at % 2 == 1))
         def _():
-            @pl.when(j + 1 < NC)
-            def _():
-                make_gates(layer, j + 1, jnp.where(second, NC, 3 * NC) + j + 1, 0, 2)
-
             @pl.when(j + 1 == NC)
             def _():
                 if NC > 1:
@@ -513,7 +497,7 @@
             def _():
                 row_loads(i + 1, start)
 
-            g = dot(hid[1 + i % 2], BT[layer], ((1,), (1,))).astype(BF)
+            g = dot(hid[1 + i % 2], B[layer], ((1,), (0,))).astype(BF)
             for p in range(ND):
                 for e in range(8):
                     own[t % SLOTS, e % 2, e // 2, p * RD : (p + 1) * RD] = g[e * RD : (e + 1) * RD, p * C : (p + 1) * C]
@@ -542,9 +526,12 @@
 
             into_layer_1(i - PAIRS)
 
-        @pl.when((at >= DOWN) & second & (i >= PAIRS + 2) & (i < PAIRS + 4))
-        def _():
-            make_gates(0, 0, 3 * NC, i - PAIRS - 2, i - PAIRS - 1)
+        last = second & (i == PAIRS + 2)
+
+        @pl.when(((at < DOWN) & (at % 2 == 1) & (j + 1 < NC)) | last)
+        def _():
+            n = jnp.where(second, NC, 3 * NC) + j + 1
+            make_gates(jnp.where(last, 0, layer), jnp.where(last, 0, j + 1), jnp.where(last, 3 * NC, n))
 
     @pl.when(c == 0)
     def _():
@@ -555,7 +542,8 @@
         L[:, CHIPS - 1] = jnp.zeros((SLOTS, RB, C), BF)
 
     forward()
-    make_gates(1, 0, NC, 0, 2)
+    load(dy_ref, B.at[1], dy_sem).wait()
+    make_gates(1, 0, NC)
     pl.semaphore_wait(barrier, 1 + jnp.where(c > 0, 1, 0) + jnp.where(c < CHIPS - 1, 1, 0))
 
     @pl.loop(0, Q + FIRST + (HOP + SPREAD) * (CHIPS - 1) + 3)
@@ -583,9 +571,9 @@
         + (jax.ShapeDtypeStruct((FF, T // 2), BF),) * 2,
         in_specs=[hbm] * 11,
         out_specs=(hbm,) * 6,
-        scratch_shapes=[pltpu.VMEM((2, D, T), BF)] * 2
+        scratch_shapes=[pltpu.VMEM((2, D, T), BF), pltpu.VMEM((2, T, D), BF), pltpu.VMEM((D, T), BF)]
         + [pltpu.VMEM((D, T), F32)]
-        + [pltpu.VMEM((ROWS, min(T, 256), D), BF)]
+        + [pltpu.VMEM((ROWS, min(T // 4, 256), D), BF)]
         + [pltpu.VMEM((3, C, T), BF)]
         + [pltpu.VMEM((2, C, T), BF)] * 2
         + [pltpu.VMEM((2, D, C), BF)] * 2
@@ -598,7 +586,7 @@
         + [pltpu.VMEM((KEPT, RB, C), BF)]
         + [dma(SLOTS)] * 2
         + [dma(SLOTS, CHIPS)] * 10
-        + [dma(2, 3), dma(2, 8), dma(2, 3), dma(KEPT, 3, ND), dma(KEPT, 3), dma(ROWS)],
+        + [dma(2, 3), dma(2, 8), dma(2, 3), dma(KEPT, 3, ND), dma(KEPT, 3), dma(ROWS), pltpu.SemaphoreType.DMA],
         compiler_params=pltpu.CompilerParams(collective_id=0, has_side_effects=True, vmem_limit_bytes=67043328),
         name="step",
     )(*arrays)[:3]

time: 499 us -> 488 us (0.978)
  Pallas kernels: 498 us -> 487 us
    pallas_call x1, Pallas kernels: 463 us -> 452 us  [mega(): pl.pallas_call(functools.partial(kernel, dims), out_shape=(jax.ShapeDtype...]
where the time goes in v3:
time: 488 us
  Pallas kernels  487 us (100%)
    pallas_call x1, Pallas kernels, mega(): pl.pallas_call(functools.partial(kernel, dims), out_shape=(jax.ShapeDtype...  452 us
    pallas_call x1, Pallas kernels, place(): pl.pallas_call(functools.partial(place_kernel, dims), in_specs=[hbm] * 3,...  35.2 us

profile of v3, /device:TPU:0, one launch (start us, length us, event | category | flops | bytes accessed | tf_op | source)
XLA Modules:
  0.0 487.8 jit_solution(2958430824582719759)
XLA Ops:
  0.6 451.7 %step.1 = (bf16[66,8,128,256]{3,2,1,0:T(8,128)(2,1)}, f32[66,128,256]{2,1,0:T(8,128)}, f32[66,128,256]{2,1,0:T(8,128)}, bf16[2816,2048]{1,0:T(8,128)(2,1)}, bf16...) custom-call(bf16[2048,1024]{1,0:T(8,128)(2,1)} %bitcast.5, bf16[2048,1024]{1,0:T(8,128)(2,1)} %bitcast.6, ...), custom_call_target="tpu_custom_call" | custom-call | tf_op jit(solution)/shard_map/step/pallas_call | solution.py:563
  452.4 35.2 %place.1 = (bf16[2,8,128,2816]{3,2,1,0:T(8,128)(2,1)}, bf16[2,8,128,2816]{3,2,1,0:T(8,128)(2,1)}, bf16[2,8,352,1024]{3,2,1,0:T(8,128)(2,1)}, f32[2,128,2816]{2,1...) custom-call(bf16[66,8,128,256]{3,2,1,0:T(8,128)(2,1)} %get-tuple-ele, ...), custom_call_target="tpu_custom_call" | custom-call | tf_op jit(solution)/shard_map/place/pallas_call | solution.py:653

commit v4 on v3

--- a/solution.py
+++ b/solution.py
@@ -13,9 +13,9 @@
 FIRST = 1
 HOP = 1
 SPREAD = 2
-SLOTS = 10
+SLOTS = 9
 ROWS = 4
-RING = 16
+RING = 12
 KEPT = 3
 
 
@@ -43,17 +43,16 @@
     wp_ref, mp_ref, vp_ref, hid2_ref, dg2_ref, du2_ref = refs[11:17]
     (AT, B, H, acc, rows, hid, dg, du, wgc, wuc, wdc, own, ex, R, L, mi, vi, wi, mo, vo, wo) = refs[17:38]
     (ex_s, ex_r, R_s, R_r, L_s, L_r, AR_s, AR_r, AL_s, AL_r, AD_s, AD_r) = refs[38:50]
-    (w_sem, row_sem, out_sem, in_sem, put_sem, x_sem, dy_sem) = refs[50:]
+    (w_sem, row_sem, out_sem, in_sem, put_sem, x_sem, dy_sem, turned, turned_down) = refs[50:]
 
     NC = FF // C
     Q = 6 * NC
     RB, RD, ND = D // 8, C // 8, D // C
     PAIRS = (NC + 1) // 2
-    assert PAIRS + 3 <= NC
+    assert PAIRS + 4 <= NC
     DOWN, HALF = 2 * NC, 3 * NC
     TT = T // 2
     TR, TS = min(T // 4, 256), min(TT, 256)
-    later = pl.ds(TT, TT)
     parts = [slice(n * C, (n + 1) * C) for n in range(ND)]
 
     me = lax.axis_index("dp")
@@ -201,25 +200,22 @@
                 L_copy(p, b).wait_recv()
                 L[s, b] = (terms + L[s, b].astype(F32)).astype(BF)
 
-        for n in range(CHIPS - 1):
+        def hop(n, act_up, act_down):
             b = CHIPS - 1 - n
-            go_up, go_down = is_q & (b > c), is_p & (n < c)
-
-            @pl.when(go_up)
-            def _():
-                up_sum(b)
-
-            @pl.when(go_down)
-            def _():
-                down_sum(n)
-
-            @pl.when(go_up)
-            def _():
-                R_copy(q, b).start()
-
-            @pl.when(go_down)
-            def _():
-                L_copy(p, n).start()
+
+            @pl.when(is_q & (b > c))
+            def _():
+                act_up(b)
+
+            @pl.when(is_p & (n < c))
+            def _():
+                act_down(n)
+
+        for n in range(CHIPS):
+            if n < CHIPS - 1:
+                hop(n, up_sum, down_sum)
+            if n > 0:
+                hop(n - 1, lambda b: R_copy(q, b).start(), lambda b: L_copy(p, b).start())
 
         q_e, gone_e = chunk(t - FIRST - HOP * (CHIPS - 1) - 2)
 
@@ -326,8 +322,8 @@
     def spills(j, act):
         s, at = j % 2, chunk_of(j)
         act(load(hid.at[s], hid2_ref.at[at], out_sem.at[s, 0]))
-        act(load(dg.at[s, :, later], dg2_ref.at[at], out_sem.at[s, 1]))
-        act(load(du.at[s, :, later], du2_ref.at[at], out_sem.at[s, 2]))
+        act(load(dg.at[s], dg2_ref.at[at], out_sem.at[s, 1]))
+        act(load(du.at[s], du2_ref.at[at], out_sem.at[s, 2]))
 
     def row_loads(i, act):
         for d in range(8):
@@ -335,20 +331,19 @@
             act(load(hid2_ref.at[at], hid.at[1 + i % 2, pl.ds(d * RD, RD)], row_sem.at[i % 2, d]))
 
     def back_loads(i, act):
-        act(load(dg2_ref.at[chunk_of(i)], dg.at[i % 2, :, later], out_sem.at[i % 2, 1]))
-        act(load(du2_ref.at[chunk_of(i)], du.at[i % 2, :, later], out_sem.at[i % 2, 2]))
+        act(load(dg2_ref.at[chunk_of(i)], dg.at[i % 2], out_sem.at[i % 2, 1]))
+        act(load(du2_ref.at[chunk_of(i)], du.at[i % 2], out_sem.at[i % 2, 2]))
 
     def token_load(i, act):
         act(load(x_ref.at[columns(i, TR)], rows.at[i % ROWS], x_sem.at[i % ROWS]))
 
     def forward():
-        quarters = range(4)
-        TQ = T // 4
-
-        def take_in(n):
-            for i in range(n * (TQ // TR), (n + 1) * (TQ // TR)):
+        def tiles(n, size):
+            return range(n * (size // TR), (n + 1) * (size // TR))
+
+        def take_in(n, size):
+            for i in tiles(n, size):
                 cols = slice(i * TR, (i + 1) * TR)
-                token_load(i, wait)
                 total = jnp.zeros((1, TR), F32)
                 for part in parts:
                     h = rows[i % ROWS, :, part].T
@@ -357,21 +352,32 @@
                 scale = lax.rsqrt(total / D + 1e-6)
                 for part in parts:
                     AT[0, part, cols] = (AT[1, part, cols].astype(F32) * scale).astype(BF)
-                if i + ROWS < T // TR:
-                    token_load(i + ROWS, start)
-
-        def hidden(j, n):
-            now = slice(n * TQ, (n + 1) * TQ)
-            gate = dot(wgc[j % 2], AT[0, :, now], ((0,), (0,)))
-            up = dot(wuc[j % 2], AT[0, :, now], ((0,), (0,)))
+
+        FIRST_CHUNK = 0
+
+        def turn():
+            turned[0], turned[1] = wgc[0].T, wuc[0].T
+            turned_down[...] = wdc[0].T
+
+        def hidden(j, n, size):
+            now = slice(n * size, (n + 1) * size)
+            if j is FIRST_CHUNK:
+                gate = dot(turned[0], AT[0, :, now], ((1,), (0,)))
+                up = dot(turned[1], AT[0, :, now], ((1,), (0,)))
+            else:
+                gate = dot(wgc[j % 2], AT[0, :, now], ((0,), (0,)))
+                up = dot(wuc[j % 2], AT[0, :, now], ((0,), (0,)))
             hid[0, :, now] = (gate * jax.nn.sigmoid(gate) * up).astype(BF)
 
-        def add(j, n):
-            now = slice(n * TQ, (n + 1) * TQ)
-            acc[:, now] = jnp.where(j > 0, acc[:, now], 0.0) + dot(wdc[j % 2], hid[0, :, now], ((0,), (0,)))
-
-        def leave(n):
-            for i in range(n * (TQ // TR), (n + 1) * (TQ // TR)):
+        def add(j, n, size):
+            now = slice(n * size, (n + 1) * size)
+            if j is FIRST_CHUNK:
+                acc[:, now] = dot(turned_down[...], hid[0, :, now], ((1,), (0,)))
+            else:
+                acc[:, now] = acc[:, now] + dot(wdc[j % 2], hid[0, :, now], ((0,), (0,)))
+
+        def leave(n, size):
+            for i in tiles(n, size):
                 cols = slice(i * TR, (i + 1) * TR)
                 total = jnp.zeros((1, TR), F32)
                 for part in parts:
@@ -382,12 +388,6 @@
                 for part in parts:
                     AT[1, part, cols] = (H[part, cols].astype(F32) * scale).astype(BF)
 
-        def staggered(steps):
-            for n in range(4 + len(steps) - 1):
-                for behind, step in enumerate(steps):
-                    if n - behind in quarters:
-                        step(n - behind)
-
         def weights(j, act):
             gate_loads(0, j, j, act)
             down_load(0, j, j, act)
@@ -395,21 +395,49 @@
         for i in range(min(ROWS, T // TR)):
             token_load(i, start)
         weights(0, start)
-        load(dy_ref, B.at[1], dy_sem).start()
-        weights(0, wait)
-        weights(1, start)
-        staggered((take_in, functools.partial(hidden, 0), functools.partial(add, 0)))
+        FA, FZ = 4, 8
+        FINE_A = T // FA
+        for n in range(FA + 2):
+            if n < FA:
+                for i in tiles(n, FINE_A):
+                    token_load(i, wait)
+                take_in(n, FINE_A)
+            if n == 1:
+                weights(0, wait)
+                turn()
+            if 1 <= n < FA + 1:
+                hidden(FIRST_CHUNK, n - 1, FINE_A)
+            if n >= 2:
+                add(FIRST_CHUNK, n - 2, FINE_A)
+            if n < FA:
+                for i in tiles(n, FINE_A):
+                    if i + ROWS < T // TR:
+                        token_load(i + ROWS, start)
+            if n == 0:
+                load(dy_ref, B.at[1], dy_sem).start()
+                weights(1, start)
 
         @pl.loop(1, NC - 1)
         def _(j):
             weights(j, wait)
             weights(j + 1, start)
-            staggered((functools.partial(hidden, j), functools.partial(add, j)))
+            for n in range(5):
+                if n < 4:
+                    hidden(j, n, T // 4)
+                if n > 0:
+                    add(j, n - 1, T // 4)
 
         weights(NC - 1, wait)
         gate_loads(1, 0, NC, start)
         down_load(1, 0, NC, start)
-        staggered((functools.partial(hidden, NC - 1), functools.partial(add, NC - 1), leave))
+        FINE_Z = T // FZ
+        for n in range(FZ + 2):
+            if n < FZ:
+                hidden(NC - 1, n, FINE_Z)
+            if 1 <= n < FZ + 1:
+                add(NC - 1, n - 1, FINE_Z)
+            if n >= 2:
+                leave(n - 2, FINE_Z)
 
     def make_gates(layer, j, n):
         s = j % 2
@@ -434,11 +462,11 @@
 
         spills(j, start)
 
-    def into_normed(i, n, half):
+    def into_normed(i, n, half, fresh):
         cols = columns(half, TT)
         from_gate = dot(wgc[n % 2], dg[i % 2, :, cols], ((1,), (0,)))
         from_up = dot(wuc[n % 2], du[i % 2, :, cols], ((1,), (0,)))
-        acc[:, cols] = jnp.where(i > 0, acc[:, cols], 0.0) + (from_gate + from_up)
+        acc[:, cols] = jnp.where(fresh, 0.0, acc[:, cols]) + (from_gate + from_up)
 
     def into_layer_1(half):
         @pl.loop(0, TT // TS)
@@ -470,9 +498,9 @@
             ex_copy(t).start()
             ex_copy(t + 1).start()
 
-            @pl.when(second)
-            def _():
-                into_normed(j, NC + j, 0)
+            @pl.when(second & (j >= 2))
+            def _():
+                into_normed(j, NC + j, 0, j == 2)
 
         @pl.when((at < DOWN) & (at % 2 == 1))
         def _():
@@ -503,30 +531,42 @@
                     own[t % SLOTS, e % 2, e // 2, p * RD : (p + 1) * RD] = g[e * RD : (e + 1) * RD, p * C : (p + 1) * C]
             ex_copy(t).start()
 
-        @pl.when((at >= DOWN) & second & (i < PAIRS))
+        @pl.when((at >= DOWN) & second & (i == 0))
         def _():
             for n in range(2):
-                @pl.when(2 * i + n < NC)
+                gate_loads(1, n, n, wait)
+                back_loads(n, wait)
+                into_normed(n, n, 0, False)
+
+        @pl.when((at >= DOWN) & second & (i >= 1) & (i <= PAIRS))
+        def _():
+            for n in range(2):
+                x = 2 * (i - 1) + n
+
+                @pl.when(x < NC)
                 def _():
-                    gate_loads(1, 2 * i + n, n, wait)
-                    back_loads(2 * i + n, wait)
-                    into_normed(2 * i + n, n, 1)
-
-                @pl.when(2 * i + n + 2 < NC)
+                    @pl.when(x >= 2)
+                    def _():
+                        gate_loads(1, x, n, wait)
+                        back_loads(x, wait)
+
+                    into_normed(x, n, 1, x == 0)
+
+                @pl.when(x + 2 < NC)
                 def _():
-                    gate_loads(1, 2 * i + n + 2, n, start)
-                    back_loads(2 * i + n + 2, start)
-
-        @pl.when((at >= DOWN) & second & (i >= PAIRS) & (i < PAIRS + 2))
-        def _():
-            @pl.when(i == PAIRS)
+                    gate_loads(1, x + 2, n, start)
+                    back_loads(x + 2, start)
+
+        @pl.when((at >= DOWN) & second & (i > PAIRS) & (i <= PAIRS + 2))
+        def _():
+            @pl.when(i == PAIRS + 1)
             def _():
                 gate_loads(0, 0, 3 * NC, start)
                 down_load(0, 0, 3 * NC, start)
 
-            into_layer_1(i - PAIRS)
-
-        last = second & (i == PAIRS + 2)
+            into_layer_1(i - PAIRS - 1)
+
+        last = second & (i == PAIRS + 3)
 
         @pl.when(((at < DOWN) & (at % 2 == 1) & (j + 1 < NC)) | last)
         def _():
@@ -567,8 +607,7 @@
             jax.ShapeDtypeStruct((Q, RB, C), F32),
             jax.ShapeDtypeStruct((Q, RB, C), F32),
         )
-        + (jax.ShapeDtypeStruct((FF, T), BF),)
-        + (jax.ShapeDtypeStruct((FF, T // 2), BF),) * 2,
+        + (jax.ShapeDtypeStruct((FF, T), BF),) * 3,
         in_specs=[hbm] * 11,
         out_specs=(hbm,) * 6,
         scratch_shapes=[pltpu.VMEM((2, D, T), BF), pltpu.VMEM((2, T, D), BF), pltpu.VMEM((D, T), BF)]
@@ -586,7 +625,8 @@
         + [pltpu.VMEM((KEPT, RB, C), BF)]
         + [dma(SLOTS)] * 2
         + [dma(SLOTS, CHIPS)] * 10
-        + [dma(2, 3), dma(2, 8), dma(2, 3), dma(KEPT, 3, ND), dma(KEPT, 3), dma(ROWS), pltpu.SemaphoreType.DMA],
+        + [dma(2, 3), dma(2, 8), dma(2, 3), dma(KEPT, 3, ND), dma(KEPT, 3), dma(ROWS), pltpu.SemaphoreType.DMA]
+        + [pltpu.VMEM((2, C, D), BF), pltpu.VMEM((D, C), BF)],
         compiler_params=pltpu.CompilerParams(collective_id=0, has_side_effects=True, vmem_limit_bytes=67043328),
         name="step",
     )(*arrays)[:3]
@@ -597,7 +637,7 @@
     NC, RB, RD, ND = FF // C, D // 8, C // 8, D // C
     Q, HALF, DOWN = 6 * NC, 3 * NC, 2 * NC
     ins, outs, bufs, (in_sem, out_sem) = refs[:3], refs[3:12], refs[12:15], refs[15:]
-    RING, LAG = bufs[0].shape[0], bufs[0].shape[0] // 2
+    RING, LAG = bufs[0].shape[0], bufs[0].shape[0] * 2 // 3
 
     def copy_in(q, n):
         return pltpu.make_async_copy(ins[n].at[q], bufs[n].at[q % RING], in_sem.at[q % RING, n])

time: 488 us -> 486 us (level)
  no operation moved by 1% of the time
where the time goes in v4:
time: 486 us
  Pallas kernels  485 us (100%)
    pallas_call x1, Pallas kernels, mega(): pl.pallas_call(functools.partial(kernel, dims), out_shape=(jax.ShapeDtype...  450 us
    pallas_call x1, Pallas kernels, place(): pl.pallas_call(functools.partial(place_kernel, dims), in_specs=[hbm] * 3,...  35 us

profile of v4, /device:TPU:0, one launch (start us, length us, event | category | flops | bytes accessed | tf_op | source)
XLA Modules:
  0.0 486.1 jit_solution(17037999023507255782)
XLA Ops:
  0.6 450.3 %step.1 = (bf16[66,8,128,256]{3,2,1,0:T(8,128)(2,1)}, f32[66,128,256]{2,1,0:T(8,128)}, f32[66,128,256]{2,1,0:T(8,128)}, bf16[2816,2048]{1,0:T(8,128)(2,1)}, bf16...) custom-call(bf16[2048,1024]{1,0:T(8,128)(2,1)} %bitcast.5, bf16[2048,1024]{1,0:T(8,128)(2,1)} %bitcast.6, ...), custom_call_target="tpu_custom_call" | custom-call | tf_op jit(solution)/shard_map/step/pallas_call | solution.py:603
  451.0 35.0 %place.1 = (bf16[2,8,128,2816]{3,2,1,0:T(8,128)(2,1)}, bf16[2,8,128,2816]{3,2,1,0:T(8,128)(2,1)}, bf16[2,8,352,1024]{3,2,1,0:T(8,128)(2,1)}, f32[2,128,2816]{2,1...) custom-call(bf16[66,8,128,256]{3,2,1,0:T(8,128)(2,1)} %get-tuple-ele, ...), custom_call_target="tpu_custom_call" | custom-call | tf_op jit(solution)/shard_map/place/pallas_call | solution.py:693
